TPU v7x, 8 devices: a whole 2x2x1 slice. The times are simulated.
8 devices in a mesh: replica: 2 (over z, y), data: 4 (over x, core).
Axes of the slice: x: 2, y: 2, z: 1, core: 2. Of those that a mesh axis runs over, the one named last changes fastest.
Arguments:
- x_seq: bfloat16 [256, 16, 512], P(('replica', 'data'))
- dy_seq: float32 [256, 16, 512], P(('replica', 'data'))
- w_stack: bfloat16 [2, 1024, 2048], replicated
- b_stack: float32 [2, 2048], replicated
Outputs:
- output 1: float32 [2, 1024, 2048], replicated
- output 2: float32 [2, 2048], replicated
- output 3: float32 [256, 16, 512], P(('replica', 'data'))
All inputs are finite; a program needn't handle non-finite values.
Results may differ from a plain program's by a relative error of at most 0.0120277.
Values are sent between devices in bfloat16 or wider.
A program may use at most 1 GiB of HBM per device.

v0:
```python
import jax
import jax.numpy as jnp
from jax import lax
from jax.sharding import PartitionSpec as P


def layer_forward(u_seq, w_layer, b_layer):
    hidden = u_seq.shape[-1]
    batch_rows = u_seq.shape[1]
    w_rec = w_layer[hidden:]
    in_proj = jnp.einsum('tbh,hg->tbg', u_seq, w_layer[:hidden], preferred_element_type=jnp.float32) + b_layer

    def time_step(carry_state, z_in):
        h_prev, c_prev = carry_state
        z_all = z_in + jnp.dot(h_prev, w_rec, preferred_element_type=jnp.float32)
        z_i, z_f, z_g, z_o = jnp.split(z_all, 4, axis=-1)
        gate_i = jax.nn.sigmoid(z_i)
        gate_f = jax.nn.sigmoid(z_f)
        gate_g = jnp.tanh(z_g)
        gate_o = jax.nn.sigmoid(z_o)
        c_new = gate_f * c_prev + gate_i * gate_g
        tanh_c = jnp.tanh(c_new)
        h_new = (gate_o * tanh_c).astype(jnp.bfloat16)
        return (h_new, c_new), (h_new, c_new, tanh_c, gate_i, gate_f, gate_g, gate_o)

    init_state = (jnp.zeros((batch_rows, hidden), jnp.bfloat16), jnp.zeros((batch_rows, hidden), jnp.float32))
    return lax.scan(time_step, init_state, in_proj)[1]


def layer_backward(u_seq, w_layer, saved_acts, dh_seq):
    hidden = u_seq.shape[-1]
    h_seq, c_seq, tanh_seq, i_seq, f_seq, g_seq, o_seq = saved_acts
    h_prev_seq = jnp.concatenate([jnp.zeros_like(h_seq[:1]), h_seq[:-1]], axis=0)
    c_prev_seq = jnp.concatenate([jnp.zeros_like(c_seq[:1]), c_seq[:-1]], axis=0)
    w_rec = w_layer[hidden:]

    def time_step(carry_state, step_in):
        dh_rec, dc_next = carry_state
        dh_out, c_prev, tanh_c, gate_i, gate_f, gate_g, gate_o = step_in
        dh_tot = dh_out + dh_rec
        dc_cur = dc_next + dh_tot * gate_o * (1.0 - tanh_c * tanh_c)
        dz_all = jnp.concatenate([dc_cur * gate_g * gate_i * (1.0 - gate_i), dc_cur * c_prev * gate_f * (1.0 - gate_f), dc_cur * gate_i * (1.0 - gate_g * gate_g), dh_tot * tanh_c * gate_o * (1.0 - gate_o)], axis=-1)
        dz_low = dz_all.astype(jnp.bfloat16)
        dh_prev = jnp.einsum('bg,hg->bh', dz_low, w_rec, preferred_element_type=jnp.float32)
        return (dh_prev, dc_cur * gate_f), (dz_low, jnp.sum(dz_all, axis=0))

    init_state = (jnp.zeros_like(dh_seq[0]), jnp.zeros_like(dh_seq[0]))
    dz_seq, db_steps = lax.scan(time_step, init_state, (dh_seq, c_prev_seq, tanh_seq, i_seq, f_seq, g_seq, o_seq), reverse=True)[1]
    dx_seq = jnp.einsum('tbg,hg->tbh', dz_seq, w_layer[:hidden], preferred_element_type=jnp.float32)
    dw_in = jnp.einsum('tbh,tbg->hg', u_seq, dz_seq, preferred_element_type=jnp.float32)
    dw_rec = jnp.einsum('tbh,tbg->hg', h_prev_seq, dz_seq, preferred_element_type=jnp.float32)
    return jnp.concatenate([dw_in, dw_rec], axis=0), jnp.sum(db_steps, axis=0), dx_seq


def reduce_weights(dw_part):
    part_low = dw_part.astype(jnp.bfloat16)
    shard_sum = lax.psum_scatter(part_low, 'data', scatter_dimension=0, tiled=True)
    shard_sum = lax.psum(shard_sum, 'replica')
    return lax.all_gather(shard_sum, 'data', axis=0, tiled=True).astype(jnp.float32)


def solution(mesh):
    batch_axes = ('replica', 'data')

    def local_grads(x_loc, dy_loc, w_stack, b_stack):
        layers = w_stack.shape[0]
        u_seq = jnp.swapaxes(x_loc, 0, 1)
        layer_inputs = []
        layer_saved = []
        for layer_idx in range(layers):
            saved_acts = layer_forward(u_seq, w_stack[layer_idx], b_stack[layer_idx])
            layer_inputs.append(u_seq)
            layer_saved.append(saved_acts)
            u_seq = saved_acts[0]
        dh_seq = jnp.swapaxes(dy_loc, 0, 1)
        dw_list = []
        db_list = []
        for layer_idx in reversed(range(layers)):
            dw_part, db_part, dh_seq = layer_backward(layer_inputs[layer_idx], w_stack[layer_idx], layer_saved[layer_idx], dh_seq)
            dw_list.append(reduce_weights(dw_part))
            db_list.append(lax.psum(db_part.astype(jnp.bfloat16), batch_axes).astype(jnp.float32))
        return jnp.stack(dw_list[::-1]), jnp.stack(db_list[::-1]), jnp.swapaxes(dh_seq, 0, 1)

    return jax.shard_map(local_grads, mesh=mesh, in_specs=(P(batch_axes), P(batch_axes), P(), P()), out_specs=(P(), P(), P(batch_axes)), check_vma=False)
```

profile of v0, /device:TPU:0, one launch (start us, length us, event | category | flops | bytes accessed | tf_op | source)
XLA Modules:
  0.0 587.3 jit_solution(570913882893854458)
XLA Ops:
  8.1 4.1 slice_bitcast_fusion
  12.2 5.0 convolution_add_fusion.3
  23.8 45.2 %while.96 = (s32[]{:T(128)}, bf16[32,512]{1,0:T(8,128)(2,1)S(1)}, f32[32,512]{1,0:T(8,128)S(1)}, bf16[16,32,512]{2,1,0:T(8,128)(2,1)}, f32[16,32,512]{2,1,0:T(8,...) while((s32[]{:T(128)}, bf16[32,512]{1,0:T(8,128)(2,1)S(1)}, ...), condition=%wide.region_1.2_spmd.clone, body=%wide.region_0.1_spmd.clone.sunk | while | flops 67485696 | bytes 3703960 | solution.py:27
  69.1 5.0 convolution_add_fusion.2
  81.8 65.5 %while.97 = (s32[]{:T(128)}, bf16[32,512]{1,0:T(8,128)(2,1)S(1)}, f32[32,512]{1,0:T(8,128)S(1)}, bf16[16,32,512]{2,1,0:T(8,128)(2,1)}, f32[16,32,512]{2,1,0:T(8,...) while((s32[]{:T(128)}, bf16[32,512]{1,0:T(8,128)(2,1)S(1)}, ...), condition=%wide.region_3.4_spmd.clone, body=%wide.region_2.3_spmd.clone.sunk | while | flops 67485696 | bytes 3704468 | solution.py:27
  81.8 2.1 convolution_add_fusion.7
  85.9 2.1 convolution_add_fusion.7
  90.0 2.1 convolution_add_fusion.7
  94.1 2.1 convolution_add_fusion.7
  98.2 2.1 convolution_add_fusion.7
  102.2 2.1 convolution_add_fusion.7
  106.3 2.1 convolution_add_fusion.7
  110.4 2.1 convolution_add_fusion.7
  114.5 2.1 convolution_add_fusion.7
  118.6 2.1 convolution_add_fusion.7
  122.7 2.1 convolution_add_fusion.7
  126.8 2.1 convolution_add_fusion.7
  130.9 2.1 convolution_add_fusion.7
  135.0 2.1 convolution_add_fusion.7
  139.1 2.1 convolution_add_fusion.7
  143.2 2.1 convolution_add_fusion.7
  153.7 114.5 %while.98 = (s32[]{:T(128)}, f32[32,512]{1,0:T(8,128)S(1)}, f32[32,512]{1,0:T(8,128)}, bf16[16,32,2048]{2,1,0:T(8,128)(2,1)}, f32[16,2048]{1,0:T(8,128)}, /*inde...) while((s32[]{:T(128)}, f32[32,512]{1,0:T(8,128)S(1)}, ...), condition=%wide.region_6.7_spmd.clone, body=%wide.region_4.6_spmd.clone.sunk | while | flops 68876288 | bytes 4284603 | solution.py:48
  154.7 1.6 convert_bitcast_fusion.13
  158.5 2.3 fusion.117
  161.8 1.6 convert_bitcast_fusion.13
  165.6 2.3 fusion.117
  169.0 1.6 convert_bitcast_fusion.13
  172.8 2.3 fusion.117
  176.2 1.6 convert_bitcast_fusion.13
  180.0 2.3 fusion.117
  183.3 1.6 convert_bitcast_fusion.13
  187.1 2.3 fusion.117
  190.5 1.6 convert_bitcast_fusion.13
  194.3 2.3 fusion.117
  197.6 1.6 convert_bitcast_fusion.13
  201.4 2.3 fusion.117
  204.8 1.6 convert_bitcast_fusion.13
  208.6 2.3 fusion.117
  212.0 1.6 convert_bitcast_fusion.13
  215.7 2.3 fusion.117
  219.1 1.6 convert_bitcast_fusion.13
  222.9 2.3 fusion.117
  226.3 1.6 convert_bitcast_fusion.13
  230.1 2.3 fusion.117
  237.2 2.3 fusion.117
  244.4 2.3 fusion.117
  251.5 2.3 fusion.117
  258.7 2.3 fusion.117
  265.9 2.3 fusion.117
  268.2 4.5 fusion.57
  272.9 1.6 broadcast.53
  275.1 78.2 %while.99 = (s32[]{:T(128)}, f32[32,512]{1,0:T(8,128)S(1)}, f32[32,512]{1,0:T(8,128)S(1)}, bf16[16,32,2048]{2,1,0:T(8,128)(2,1)}, f32[16,2048]{1,0:T(8,128)}, /*...) while((s32[]{:T(128)}, f32[32,512]{1,0:T(8,128)S(1)}, ...), condition=%wide.region_9.10_spmd.clone, body=%wide.region_7.9_spmd.clone.sunk | while | flops 68876288 | bytes 4284603 | solution.py:48
  353.4 3.2 bitcast_convert_fusion.2
  358.0 2.6 pad_maximum_fusion.2
  361.6 3.0 bitcast_convert_fusion
  366.0 2.6 pad_maximum_fusion.3
  368.6 33.3 %reduce-scatter.3.cloned.1.call-done = bf16[256,2048]{1,0:T(8,128)(2,1)} async-done(((bf16[1024,2048]{1,0:T(8,128)(2,1)}), bf16[256,2048]{1,0:T(8,128)(2,1)}) %reduce-scatter.3.cloned.1.call-update) | async-done | bytes 1048592 | tf_op jit(solution)/shard_map/reduce_scatter | solution.py:57
  401.9 41.4 %reduce-scatter.5.cloned.1.call-done = bf16[256,2048]{1,0:T(8,128)(2,1)} async-done(((bf16[1024,2048]{1,0:T(8,128)(2,1)}), bf16[256,2048]{1,0:T(8,128)(2,1)}) %reduce-scatter.5.cloned.1.call-update) | async-done | bytes 1048592 | tf_op jit(solution)/shard_map/reduce_scatter | solution.py:57
  443.4 59.4 %all-reduce.8.cloned.1.call-done = (bf16[256,2048]{1,0:T(8,128)(2,1)}, bf16[256,2048]{1,0:T(8,128)(2,1)}) async-done(((bf16[256,2048]{1,0:T(8,128)(2,1)}, bf16[256,2048]{1,0:T(8,128)(2,1)}), (bf16[256,2048]{1,0:T(8,128)(2,1)}, bf16[256,2048]{1,0:T(8,128)(2,1)})) %all-reduce.8.cloned.1.call-update) | async-done | bytes 2097168 | tf_op jit(solution)/shard_map/psum | solution.py:58
  503.5 2.9 fusion.67
  508.0 23.0 %all-reduce.4 = (bf16[1,2048]{1,0:T(2,128)(2,1)S(1)}, bf16[1,2048]{1,0:T(2,128)(2,1)S(1)}) all-reduce(bf16[1,2048]{1,0:T(2,128)(2,1)S(1)} %stack.33, bf16[1,2048]{1,0:T(2,128)(2,1)S(1)} %stack.32), channel_id=1, replica_groups=mesh['replica'=2,'data'=4] {'replica','data'}, use_global_device_ids=true, to_apply=%region_17.18 | all-reduce | flops 4096 | bytes 16384 | tf_op jit(solution)/shard_map/psum | solution.py:81
  531.7 5.5 all-gather.3.cloned.1.call-done
  537.1 32.9 %all-gather.5.cloned.1.call-done = bf16[1024,2048]{1,0:T(8,128)(2,1)} async-done(((bf16[256,2048]{1,0:T(8,128)(2,1)}), bf16[1024,2048]{1,0:T(8,128)(2,1)}) %all-gather.5.cloned.1.call-update) | async-done | bytes 4194320 | tf_op jit(solution)/shard_map/all_gather | solution.py:59
  570.0 10.7 %maximum_convert_fusion = f32[2,1024,2048]{2,1,0:T(8,128)} fusion(bf16[1,1024,2048]{2,1,0:T(8,128)(2,1)} %bitcast.279, bf16[1,1024,2048]{2,1,0:T(8,128)(2,1)} %bitcast.278), kind=kLoop, calls=%fused_computation.122 | loop fusion | flops 8388608 | bytes 25165824 | tf_op jit(solution)/shard_map/stack | solution.py:82
  (344 shorter events, 244.9 us)
Async XLA Ops:
  7.2 394.7 %reduce-scatter.3.cloned.1.call-start = ((), (), s32[]{:S(2)}) async-start(), calls=%async_computation.2 | async-start | bytes 5242880 | tf_op jit(solution)/shard_map/reduce_scatter | solution.py:57
  8.1 4.1 copy-start.7
  147.3 1.5 copy-start.2
  353.4 3.2 copy-start
  353.4 3.2 copy-start.8
  360.6 1.0 copy-start.4
  360.6 82.7 %reduce-scatter.5.cloned.1.call-start = ((), (), s32[]{:S(2)}) async-start(), calls=%async_computation.4 | async-start | bytes 5242880 | tf_op jit(solution)/shard_map/reduce_scatter | solution.py:57
  361.6 3.0 copy-start.1
  361.6 3.0 copy-start.3
  368.6 134.2 %all-reduce.8.cloned.1.call-start = ((), (), s32[]{:S(2)}) async-start(), calls=%async_computation.6 | async-start | bytes 4194304 | tf_op jit(solution)/shard_map/psum | solution.py:58
  443.3 60.1 %copy-start.6 = (f32[16,2048]{1,0:T(8,128)S(1)}, f32[16,2048]{1,0:T(8,128)}, u32[]{:S(2)}) copy-start(f32[16,2048]{1,0:T(8,128)} %get-tuple-element.667) | copy-start | bytes 393220
  443.3 60.2 %copy-start.5 = (f32[16,2048]{1,0:T(8,128)S(1)}, f32[16,2048]{1,0:T(8,128)}, u32[]{:S(2)}) copy-start(f32[16,2048]{1,0:T(8,128)} %get-tuple-element.668) | copy-start | bytes 393220
  443.3 93.8 %all-gather.3.cloned.1.call-start = ((), (), s32[]{:S(2)}) async-start(), calls=%async_computation.3 | async-start | bytes 5242880 | tf_op jit(solution)/shard_map/all_gather | solution.py:59
  502.8 67.2 %all-gather.5.cloned.1.call-start = ((), (), s32[]{:S(2)}) async-start(), calls=%async_computation.5 | async-start | bytes 5242880 | tf_op jit(solution)/shard_map/all_gather | solution.py:59
Sparse Core Ops, SparseCore 0:
  360.7 41.1 reduce-scatter.2
  405.0 38.2 reduce-scatter.4
  445.6 57.1 all-reduce.7
  504.2 32.8 all-gather.2
  538.5 31.4 all-gather.4
where the time goes:
time: 594 us; the launch traced here: 587 us
  waiting for transfers between devices  173 us (29%)
  other arithmetic  157 us (26%)
  matrix products  130 us (22%)
  local copies, waits for them, and re-layouts  88.6 us (15%)
  blocking collectives  23 us (4%)
  between operations  14 us (2%)
    reduce_scatter x2, waiting for transfers between devices, reduce_weights(): lax.psum_scatter(part_low, 'data', scatter_dimension=0, tiled=True)  74.6 us
    concatenate x64, other arithmetic, time_step(): jnp.concatenate([dc_cur * gate_g * gate_i * (1.0 - gate_i), dc_cur * c_pr...  73.9 us
    psum x1, waiting for transfers between devices, reduce_weights(): shard_sum = lax.psum(shard_sum, 'replica')  59.4 us
    dot_general x32, matrix products, time_step(): z_all = z_in + jnp.dot(h_prev, w_rec, preferred_element_type=jnp.float32)  55.5 us
    dot_general x32, matrix products, time_step(): jnp.einsum('bg,hg->bh', dz_low, w_rec, preferred_element_type=jnp.float32)  48.5 us
    dynamic_update_slice x32, local copies, waits for them, and re-layouts, layer_backward(): lax.scan(time_step, init_state, (dh_seq, c_prev_seq, tanh_seq, i_seq, f_s...  47.9 us
    dynamic_update_slice x64, other arithmetic, layer_forward(): return lax.scan(time_step, init_state, in_proj)[1]  44.8 us
    all_gather x2, waiting for transfers between devices, reduce_weights(): lax.all_gather(shard_sum, 'data', axis=0, tiled=True).astype(jnp.float32)  38.4 us
  transfers between devices with their start and end apart: 5, of which 5 were waited for; matrix products, arithmetic and copies ran while one was open for 2% of the time, Pallas kernels for 0%

commit v1 on v0

v1 whole, which is shorter than its diff:
```python
import jax
import jax.numpy as jnp
from jax import lax
from jax.experimental import pallas as pl
from jax.experimental.pallas import tpu as pltpu
from jax.sharding import PartitionSpec as P

F32, BF16 = jnp.float32, jnp.bfloat16
MESH = pl.DeviceIdType.MESH
T, B, H = 16, 32, 512
G, R = 4 * H, T * B
C = 32


def dot(a, b):
    return jnp.dot(a, b, preferred_element_type=F32)


def dot_nt(a, b):
    return lax.dot_general(a, b, (((1,), (1,)), ((), ())), preferred_element_type=F32)


def sigmoid(z):
    return 0.5 * jnp.tanh(0.5 * z) + 0.5


def rows(start, n, m=16):
    return pl.ds(start, n) if isinstance(start, int) else pl.ds(pl.multiple_of(start, m), n)


def step_kernel(x_hbm, dy_hbm, w_hbm, b_ref, res, dbo, dxo,
                xv, xf, dyv, w, wt, hb, gt, cb, tc, dz, eb, dbacc, dbs, dbb, dbr, dwb, rp, r1, r2,
                lsem, s_rp, v_rp, s_1, v_1, s_2, v_2, s_a, v_a, s_p, v_p, s_db, v_db):
    rep = lax.axis_index("replica")
    dat = lax.axis_index("data")
    mx, core = dat // 2, dat % 2
    partner = (rep, dat + 1 - 2 * core)
    x_nbr = (rep, lax.rem(dat + 2, 4))
    y_nbr = (1 - rep, dat)
    nbr = ((x_nbr, y_nbr), (y_nbr, x_nbr))
    bits = ((mx, rep), (rep, mx))

    def remote(src, dst, s, v, dev):
        return pltpu.make_async_remote_copy(src_ref=src, dst_ref=dst, send_sem=s, recv_sem=v,
                                            device_id=dev, device_id_type=MESH)

    others = [(lax.rem(rep + (d // 4), 2), lax.rem(dat + (d % 4), 4)) for d in range(1, 8)]
    barrier = pltpu.get_barrier_semaphore()
    for dev in others:
        pl.semaphore_signal(barrier, inc=1, device_id=dev, device_id_type=MESH)

    ld_x = [pltpu.make_async_copy(x_hbm.at[:, pl.ds(k * 128, 128)], xv.at[k], lsem.at[k]) for k in range(4)]
    ld_dy = [pltpu.make_async_copy(dy_hbm.at[:, pl.ds(k * 128, 128)], dyv.at[k], lsem.at[4 + k]) for k in range(4)]
    ld_w = [pltpu.make_async_copy(w_hbm.at[l, pl.ds(k * H, H), pl.ds(j * 256, 256)], w.at[l, k, j],
                                  lsem.at[8 + (2 * l + k) * 8 + j])
            for l in range(2) for k in range(2) for j in range(8)]
    for c in ld_x + ld_w + ld_dy:
        c.start()
    for c in ld_x:
        c.wait()
    xf[...] = xv[...].astype(F32)
    for l in range(2):
        hb[l + 1, pl.ds(0, B), :] = jnp.zeros((B, H), BF16)
        cb[l, pl.ds(0, B), :] = jnp.zeros((B, H), F32)

    @pl.loop(0, T)
    def _(t):
        hb[0, rows((t + 1) * B, B), :] = jnp.concatenate(
            [xf[k, pl.ds(t, B, stride=T), :] for k in range(4)], axis=1).astype(BF16)

    def in_proj(l):
        u = hb[l, pl.ds(B, R), :]
        for j in range(8):
            gt[l, j // 2, :, (j % 2) * 256:(j % 2) * 256 + 256] = dot(u, w[l, 0, j]) + b_ref[l:l + 1, j * 256:(j + 1) * 256]

    def fwd_step(l, t):
        r0, r1_ = rows(t * B, B), rows((t + 1) * B, B)
        h_prev = hb[l + 1, r0, :]
        z = [None] * 4
        for k in (0, 2, 1, 3):
            z[k] = gt[l, k, r0, :] + jnp.concatenate([dot(h_prev, w[l, 1, 2 * k + n]) for n in range(2)], axis=1)
        i, g, f, o = sigmoid(z[0]), jnp.tanh(z[2]), sigmoid(z[1]), sigmoid(z[3])
        c = f * cb[l, r0, :] + i * g
        th = jnp.tanh(c)
        for k, v in enumerate((i, f, g, o)):
            gt[l, k, r0, :] = v
        cb[l, r1_, :] = c
        tc[l, r0, :] = th
        hb[l + 1, r1_, :] = (o * th).astype(BF16)

    def transpose_rec(l):
        @pl.loop(0, 8)
        def _(j):
            for n in range(2):
                wt[l, n, rows(j * 256, 256), :] = w[l, 1, j, pl.ds(n * 256, 256), :].T

    for c in ld_w[:8]:
        c.wait()
    in_proj(0)
    for c in ld_w[8:]:
        c.wait()
    for l in range(2):
        if l:
            in_proj(l)
        pl.loop(0, T)(lambda t, l=l: fwd_step(l, t))
        transpose_rec(l)

    for c in ld_dy:
        c.wait()
    dbacc[...] = jnp.zeros_like(dbacc)

    def bwd_layer(l, e_of):
        def body(s, carry):
            r, dc_next = carry
            t = T - 1 - s
            r0 = rows(t * B, B)
            i, f, g, o = [gt[l, k, r0, :] for k in range(4)]
            th, c_prev = tc[l, r0, :], cb[l, r0, :]
            dh = e_of(t) + r
            dc = dc_next + dh * o * (1.0 - th * th)
            dzs = (dc * g * i * (1.0 - i), dc * c_prev * f * (1.0 - f), dc * i * (1.0 - g * g), dh * th * o * (1.0 - o))
            acc = None
            for k, d in enumerate(dzs):
                dbacc[l, :, k * H:(k + 1) * H] += d[0:8] + d[8:16] + d[16:24] + d[24:32]
                d16 = d.astype(BF16)
                for n in range(2):
                    dz[l, 2 * k + n, r0, :] = d16[:, n * 256:(n + 1) * 256]
                p = [dot(d16, wt[l, n, pl.ds(k * H, H), :]) for n in range(2)]
                acc = p if acc is None else [a + b for a, b in zip(acc, p)]
            return jnp.concatenate(acc, axis=1), dc * f

        zero = jnp.zeros((B, H), F32)
        lax.fori_loop(0, T, body, (zero, zero))

    def dx_of(l, put):
        acc = None
        for m in range(2):
            rr = pl.ds(m * 256, 256)
            acc = None
            for j in range(8):
                p = dot_nt(dz[l, j, rr, :], w[l, 0, j])
                acc = p if acc is None else acc + p
            put(m, acc)

    def block_row(who, q, grp):
        b1 = bits[q][0]
        part = 1 - b1 if grp == 0 else b1
        return who * H + q * 256 + part * 128

    def dw_block(l, who, q, grp):
        r0 = block_row(who, q, grp)
        lhs = hb[l + who, rows(B * (1 - who), R, B), rows(r0 - who * H, 128, 128)]
        lt = lhs.T
        for n in range(8):
            dwb[l, rows(r0, 128), n * 256:(n + 1) * 256] = dot(lt, dz[l, n]).astype(BF16)

    def cp_rp(l, q, grp):
        rr = rows(block_row(1 - core, q, grp), 128)
        return remote(dwb.at[l, rr], rp.at[l, q, grp], s_rp.at[l, q, grp], v_rp.at[l, q, grp], partner)

    def add_rows(l, r0, src, n):
        @pl.loop(0, n // 16)
        def _(i):
            rr = rows(r0 + i * 16, 16)
            dwb[l, rr, :] = (dwb[l, rr, :].astype(F32) + src[rows(i * 16, 16), :].astype(F32)).astype(BF16)

    def piece(q, i, kept):
        b1, b2 = bits[q]
        half = 1 - b2 if i < 2 else b2
        return block_row(core, q, 1 if kept else 0) + 64 * half + C * (i % 2)

    def cp_1(l, q, i):
        return remote(dwb.at[l, rows(piece(q, i, False), C)], r1.at[l, q, i], s_1.at[l, q, i], v_1.at[l, q, i], nbr[q][0])

    def cp_2(l, q, i):
        return remote(dwb.at[l, rows(piece(q, i, True), C)], r2.at[l, q, i], s_2.at[l, q, i], v_2.at[l, q, i], nbr[q][1])

    def fin_row(q, k, i):
        b1, b2 = bits[q]
        c1 = b1 if k in (0, 1) else 1 - b1
        c2 = b2 if k in (0, 2) else 1 - b2
        return core * H + q * 256 + c1 * 128 + c2 * 64 + C * i

    def cp_a(l, q, k, i):
        rr = rows(fin_row(q, 1 if k == 2 else 0, i), C)
        return remote(res.at[l, rr], res.at[l, rr], s_a.at[l, q, k, i], v_a.at[l, q, k, i], nbr[q][1 if k == 0 else 0])

    def cp_p(l, q, k, i):
        rr = rows(fin_row(q, k, i), C)
        return remote(res.at[l, rr], res.at[l, rr], s_p.at[l, q, k, i], v_p.at[l, q, k, i], partner)

    QI = [(q, i) for i in range(2) for q in range(2)]

    def grads_send(l):
        for q in range(2):
            dw_block(l, 1 - core, q, 0)
            cp_rp(l, q, 0).start()
        for q in range(2):
            dw_block(l, core, q, 0)
        for q in range(2):
            cp_rp(l, q, 0).wait_recv()
            add_rows(l, block_row(core, q, 0), rp.at[l, q, 0], 128)
            for i in range(4):
                cp_1(l, q, i).start()
        for q in range(2):
            dw_block(l, 1 - core, q, 1)
            cp_rp(l, q, 1).start()
        for q in range(2):
            dw_block(l, core, q, 1)
        for q in range(2):
            cp_rp(l, q, 1).wait_recv()
            add_rows(l, block_row(core, q, 1), rp.at[l, q, 1], 128)

    def recv_1(l, half):
        for q, i in QI:
            i += 2 * half
            cp_1(l, q, i).wait_recv()
            add_rows(l, piece(q, i, True), r1.at[l, q, i], C)
            if half == 0:
                cp_2(l, q, i).start()

    def recv_2(l):
        for q, i in QI:
            cp_2(l, q, i).wait_recv()
            src, dst = piece(q, i + 2, True), fin_row(q, 0, i)

            @pl.loop(0, C // 16)
            def _(m):
                res[l, rows(dst + m * 16, 16), :] = (
                    dwb[l, rows(src + m * 16, 16), :].astype(F32) + r2[l, q, i, rows(m * 16, 16), :].astype(F32)).astype(BF16)
            cp_a(l, q, 0, i).start()
            cp_a(l, q, 1, i).start()
            cp_p(l, q, 0, i).start()

    def recv_a1(l):
        for q, i in QI:
            cp_a(l, q, 0, i).wait_recv()
            cp_a(l, q, 2, i).start()
            cp_p(l, q, 1, i).start()

    def recv_a2(l, k):
        for q, i in QI:
            cp_a(l, q, k, i).wait_recv()
            cp_p(l, q, k + 1, i).start()

    bwd_layer(1, lambda t: jnp.concatenate([dyv[k, pl.ds(t, B, stride=T), :] for k in range(4)], axis=1))
    pl.semaphore_wait(barrier, 7)
    grads_send(1)

    def put_e(m, v):
        eb[pl.ds(m * 256, 256), :] = v
    dx_of(1, put_e)
    bwd_layer(0, lambda t: eb[rows(t * B, B), :])
    recv_1(1, 0)
    grads_send(0)

    for l in range(2):
        for j in range(8):
            dbs[8 * l + j:8 * l + j + 1, :] = jnp.sum(dbacc[l, :, j * 256:(j + 1) * 256], axis=0, keepdims=True)
    dbb[...] = dbs[...].astype(BF16)
    me = rep * 4 + dat
    cps = [remote(dbb, dbr.at[d - 1], s_db.at[d - 1], v_db.at[d - 1], dev) for d, dev in enumerate(others, 1)]
    for c in cps:
        c.start()

    def put_dx(m, v):
        for s in range(8):
            for k in range(4):
                dxo[k, pl.ds(8 * m + s, B, stride=T), :] = v[s * B:(s + 1) * B, k * 128:(k + 1) * 128]
    dx_of(0, put_dx)

    recv_1(1, 1)
    recv_2(1)
    recv_a1(1)
    recv_1(0, 0)
    recv_1(0, 1)
    recv_a2(1, 1)
    recv_a2(1, 2)
    recv_2(0)
    recv_a1(0)
    for c in cps:
        c.wait_recv()
    tot = dbb[...].astype(F32)
    for d in range(7):
        tot += dbr[d].astype(F32)
    dbo[...] = tot
    recv_a2(0, 1)
    recv_a2(0, 2)
    for l in (1, 0):
        for q in range(2):
            for grp in range(2):
                cp_rp(l, q, grp).wait_send()
            for i in range(4):
                cp_1(l, q, i).wait_send()
            for i in range(2):
                cp_2(l, q, i).wait_send()
                for k in range(3):
                    cp_a(l, q, k, i).wait_send()
                for k in range(4):
                    cp_p(l, q, k, i).wait_send()
                    cp_p(l, q, k, i).wait_recv()
    for c in cps:
        c.wait_send()


def out_kernel(res, dbo, dxo, dw_ref, db_ref, dx_ref, buf, sem, xsem):
    cx = [pltpu.make_async_copy(dxo.at[k], dx_ref.at[:, pl.ds(k * 128, 128)], xsem.at[k]) for k in range(4)]
    for c in cx:
        c.start()
    n = 128

    def cp(s, slot):
        return pltpu.make_async_copy(buf.at[slot], dw_ref.at[s // 8, rows(lax.rem(s, 8) * n, n)], sem.at[slot])

    @pl.loop(0, 16)
    def _(s):
        slot = lax.rem(s, 4)

        @pl.when(s >= 4)
        def _():
            cp(s - 4, slot).wait()

        @pl.loop(0, n // 16)
        def _(i):
            buf[slot, rows(i * 16, 16), :] = res[s // 8, rows(lax.rem(s, 8) * n + i * 16, 16), :].astype(F32)
        cp(s, slot).start()
    for l in range(2):
        for j in range(8):
            db_ref[l:l + 1, j * 256:(j + 1) * 256] = dbo[8 * l + j:8 * l + j + 1, :]
    for s in range(12, 16):
        cp(s, s % 4).wait()
    for c in cx:
        c.wait()


def solution(mesh):
    vm = pl.BlockSpec(memory_space=pltpu.VMEM)
    hbm = pl.BlockSpec(memory_space=pl.ANY)
    dma = pltpu.SemaphoreType.DMA

    def local_step(x, dy, w, b):
        scratch = [
            pltpu.VMEM((4, R, 128), BF16), pltpu.VMEM((4, R, 128), F32), pltpu.VMEM((4, R, 128), F32),
            pltpu.VMEM((2, 2, 8, H, 256), BF16), pltpu.VMEM((2, 2, G, 256), BF16), pltpu.VMEM((3, R + B, H), BF16),
            pltpu.VMEM((2, 4, R, H), F32), pltpu.VMEM((2, R + B, H), F32), pltpu.VMEM((2, R, H), F32),
            pltpu.VMEM((2, 8, R, 256), BF16), pltpu.VMEM((R, H), F32), pltpu.VMEM((2, 8, G), F32),
            pltpu.VMEM((16, 256), F32), pltpu.VMEM((16, 256), BF16), pltpu.VMEM((7, 16, 256), BF16),
            pltpu.VMEM((2, 2 * H, G), BF16), pltpu.VMEM((2, 2, 2, 128, G), BF16),
            pltpu.VMEM((2, 2, 4, C, G), BF16), pltpu.VMEM((2, 2, 2, C, G), BF16),
            dma((40,)), dma((2, 2, 2)), dma((2, 2, 2)), dma((2, 2, 4)), dma((2, 2, 4)), dma((2, 2, 2)), dma((2, 2, 2)),
            dma((2, 2, 3, 2)), dma((2, 2, 3, 2)), dma((2, 2, 4, 2)), dma((2, 2, 4, 2)), dma((7,)), dma((7,)),
        ]
        res, dbo, dxo = pl.pallas_call(
            step_kernel,
            out_shape=(jax.ShapeDtypeStruct((2, 2 * H, G), BF16), jax.ShapeDtypeStruct((16, 256), F32),
                       jax.ShapeDtypeStruct((4, R, 128), F32)),
            in_specs=[hbm, hbm, hbm, vm], out_specs=(vm, vm, vm), scratch_shapes=scratch,
            compiler_params=pltpu.CompilerParams(collective_id=0, has_side_effects=True, vmem_limit_bytes=63 * 1024 * 1024),
        )(x.reshape(R, H), dy.reshape(R, H), w, b)
        dw, db, dx = pl.pallas_call(
            out_kernel,
            out_shape=(jax.ShapeDtypeStruct((2, 2 * H, G), F32), jax.ShapeDtypeStruct((2, G), F32),
                       jax.ShapeDtypeStruct((R, H), F32)),
            in_specs=[vm, vm, vm], out_specs=(hbm, vm, hbm),
            scratch_shapes=[pltpu.VMEM((4, 128, G), F32), dma((4,)), dma((4,))],
            compiler_params=pltpu.CompilerParams(vmem_limit_bytes=32 * 1024 * 1024),
        )(res, dbo, dxo)
        return dw, db, dx.reshape(B, T, H)

    rows_spec = P(("replica", "data"))
    return jax.shard_map(local_step, mesh=mesh, in_specs=(rows_spec, rows_spec, P(), P()),
                         out_specs=(P(), P(), rows_spec), check_vma=False)
```

time: 594 us -> 126 us (0.21); the launches traced: 587 us -> 126 us
  waiting for transfers between devices: 173 us -> 0 us
  other arithmetic: 157 us -> 0 us
  matrix products: 130 us -> 0 us
  Pallas kernels: 0 us -> 120 us
  local copies, waits for them, and re-layouts: 88.6 us -> 5.32 us
  blocking collectives: 23 us -> 0 us
  between operations: 14 us -> 0.65 us
    dot_general x72 -> x0, matrix products: 130 us -> none  [the longest x32 55.5 us: time_step(): z_all = z_in + jnp.dot(h_prev, w_rec, preferred_element_type=jnp.float32)]
    pallas_call x0 -> x2, Pallas kernels: none -> 120 us  [the longest x1 113 us: local_step(): pl.pallas_call(step_kernel, out_shape=(jax.ShapeDtypeStruct((2, 2 * H, G)...]
    concatenate x66 -> x0, other arithmetic: 79 us -> none  [the longest x64 73.9 us: time_step(): jnp.concatenate([dc_cur * gate_g * gate_i * (1.0 - gate_i), dc_cur * c_pr...]
    reduce_scatter x2 -> x0, waiting for transfers between devices: 74.6 us -> none  [reduce_weights(): lax.psum_scatter(part_low, 'data', scatter_dimension=0, tiled=True)]
    dynamic_update_slice x96 -> x0, other arithmetic: 66.1 us -> none  [the longest x64 44.8 us: layer_forward(): return lax.scan(time_step, init_state, in_proj)[1]]
    psum x1 -> x0, waiting for transfers between devices: 59.4 us -> none  [reduce_weights(): shard_sum = lax.psum(shard_sum, 'replica')]
    dynamic_update_slice x64 -> x0, local copies, waits for them, and re-layouts: 58.2 us -> none  [the longest x32 47.9 us: layer_backward(): lax.scan(time_step, init_state, (dh_seq, c_prev_seq, tanh_seq, i_seq, f_s...]
    all_gather x2 -> x0, waiting for transfers between devices: 38.4 us -> none  [reduce_weights(): lax.all_gather(shard_sum, 'data', axis=0, tiled=True).astype(jnp.float32)]
  transfers between devices with their start and end apart: 5 -> 0, of which waited for: 5 -> 0; matrix products, arithmetic and copies ran while one was open for 2% -> 0% of each run, Pallas kernels for 0% -> 0%
where the time goes in v1:
time: 126 us
  Pallas kernels  120 us (95%)
  local copies, waits for them, and re-layouts  5.32 us (4%)
    pallas_call x1, Pallas kernels, local_step(): pl.pallas_call(step_kernel, out_shape=(jax.ShapeDtypeStruct((2, 2 * H, G)...  113 us
    pallas_call x1, Pallas kernels, local_step(): pl.pallas_call(out_kernel, out_shape=(jax.ShapeDtypeStruct((2, 2 * H, G),...  6.81 us
    unnamed x6, local copies, waits for them, and re-layouts  5.32 us

profile of v1, /device:TPU:0, one launch (start us, length us, event | category | flops | bytes accessed | tf_op | source)
XLA Modules:
  0.0 125.5 jit_solution(17860562039660476880)
XLA Ops:
  0.6 112.7 %shard_map.67 = (bf16[2,1024,2048]{2,1,0:T(8,128)(2,1)}, f32[16,256]{1,0:T(8,128)}, f32[4,512,128]{2,1,0:T(8,128)}) custom-call(bf16[512,512]{1,0:T(8,128)(2,1)} %bitcast.4, f32[512,512]{1,0:T(8,128)} %bitcast.3, bf16[2,1024,2048]{2,1,0:T(8,128)(2,1)} %w_hbm.1, f32[2,2048]{1,0:T(2,128)} %b_ref.1), custom_call_target="tpu_custom_call" | custom-call | tf_op jit(solution)/shard_map/pallas_call | solution.py:353
  113.4 0.0 copy-start
  113.4 3.4 %copy-done = bf16[2,1024,2048]{2,1,0:T(8,128)(2,1)S(1)} copy-done((bf16[2,1024,2048]{2,1,0:T(8,128)(2,1)S(1)}, bf16[2,1024,2048]{2,1,0:T(8,128)(2,1)}, u32[]{:S(2)}) %copy-start) | copy-done | bytes 8388632
  116.8 0.0 copy-start.1
  116.8 1.2 copy-done.1
  118.0 0.0 copy-start.2
  118.0 0.7 copy-done.2
  118.7 6.8 %shard_map.68 = (f32[2,1024,2048]{2,1,0:T(8,128)}, f32[2,2048]{1,0:T(2,128)}, f32[512,512]{1,0:T(8,128)}) custom-call(bf16[2,1024,2048]{2,1,0:T(8,128)(2,1)S(1)} %copy-done, f32[16,256]{1,0:T(8,128)S(1)} %copy-done.2, f32[4,512,128]{2,1,0:T(8,128)S(1)} %copy-done.1), custom_call_target="tpu_custom_call" | custom-call | tf_op jit(solution)/shard_map/pallas_call | solution.py:360
Async XLA Ops:
  113.4 3.4 %copy-start = (bf16[2,1024,2048]{2,1,0:T(8,128)(2,1)S(1)}, bf16[2,1024,2048]{2,1,0:T(8,128)(2,1)}, u32[]{:S(2)}) copy-start(bf16[2,1024,2048]{2,1,0:T(8,128)(2,1)} %get-tuple-element.9.res) | copy-start | bytes 25165828
  116.8 1.2 copy-start.1
  118.0 0.7 copy-start.2

commit v2 on v1

v2 whole, which is shorter than its diff:
```python
import jax
import jax.numpy as jnp
from jax import lax
from jax.experimental import pallas as pl
from jax.experimental.pallas import tpu as pltpu
from jax.sharding import PartitionSpec as P

F32, BF16 = jnp.float32, jnp.bfloat16
MESH = pl.DeviceIdType.MESH
T, B, H = 16, 32, 512
G, R = 4 * H, T * B
ORDER = (0, 1, 2, 3)
PAD = 24
VMEM_LIMIT = 54 * 1024 * 1024
C = 64


def dot(a, b):
    return jnp.dot(a, b, preferred_element_type=F32)


def dot_nt(a, b):
    return lax.dot_general(a, b, (((1,), (1,)), ((), ())), preferred_element_type=F32)


def sigmoid(z):
    return 0.5 * jnp.tanh(0.5 * z) + 0.5


def rows(start, n, m=16):
    return pl.ds(start, n) if isinstance(start, int) else pl.ds(pl.multiple_of(start, m), n)


def step_kernel(x_hbm, dy_hbm, w_hbm, b_hbm, res, dbo, dxo,
                b_ref, xv, xf, dyv, w, wt, hb, gt, cb, tc, dz, eb, dbacc, dbs, dbb, dbr, dwb, rp, r1, r2,
                lsem, s_rp, v_rp, s_1, v_1, s_2, v_2, s_a, v_a, s_p, v_p, s_db, v_db):
    rep = lax.axis_index("replica")
    dat = lax.axis_index("data")
    mx, core = dat // 2, dat % 2
    partner = (rep, dat + 1 - 2 * core)
    x_nbr = (rep, lax.rem(dat + 2, 4))
    y_nbr = (1 - rep, dat)
    nbr = ((x_nbr, y_nbr), (y_nbr, x_nbr))
    bits = ((mx, rep), (rep, mx))

    def remote(src, dst, s, v, dev):
        return pltpu.make_async_remote_copy(src_ref=src, dst_ref=dst, send_sem=s, recv_sem=v,
                                            device_id=dev, device_id_type=MESH)

    others = [(lax.rem(rep + (d // 4), 2), lax.rem(dat + (d % 4), 4)) for d in range(1, 8)]
    barrier = pltpu.get_barrier_semaphore()

    ld_x = [pltpu.make_async_copy(x_hbm.at[:, pl.ds(k * 128, 128)], xv.at[k], lsem.at[0]) for k in range(4)]
    ld_dy = [pltpu.make_async_copy(dy_hbm.at[:, pl.ds(k * 128, 128)], dyv.at[k], lsem.at[1]) for k in range(4)]
    ld_w = [pltpu.make_async_copy(w_hbm.at[l, pl.ds(k * H, H), pl.ds(j * 256, 256)], w.at[l, k, j],
                                  lsem.at[2 + 2 * l + k])
            for l in range(2) for k in range(2) for j in range(8)]
    ld_b = pltpu.make_async_copy(b_hbm, b_ref, lsem.at[6])
    for c in ld_x + [ld_b] + ld_w[:16]:
        c.start()
    for dev in others:
        pl.semaphore_signal(barrier, inc=1, device_id=dev, device_id_type=MESH)
    for l in range(2):
        hb[l + 1, pl.ds(0, B), :] = jnp.zeros((B, H), BF16)
        cb[l, pl.ds(0, B), :] = jnp.zeros((B, H), F32)
    pltpu.make_async_copy(xv, xv, lsem.at[0]).wait()
    for i in range(B):
        xf[:, i * PAD:i * PAD + T, :] = xv[:, i * T:(i + 1) * T, :].astype(F32)

    @pl.loop(0, T)
    def _(t):
        hb[0, rows((t + 1) * B, B), :] = jnp.concatenate(
            [xf[k, pl.ds(t, B, stride=PAD), :] for k in range(4)], axis=1).astype(BF16)
    for c in ld_w[16:] + ld_dy:
        c.start()

    def wait_w(l, k):
        pltpu.make_async_copy(w.at[l, k], w.at[l, k], lsem.at[2 + 2 * l + k]).wait()

    ld_b.wait()
    wait_w(0, 0)

    def in_block(l, s, n, m=128):
        r0 = rows(s * 128, m)
        gt[l, n // 2, r0, (n % 2) * 256:(n % 2) * 256 + 256] = (
            dot(hb[l, rows(B + s * 128, m), :], w[l, 0, n]) + b_ref[l:l + 1, n * 256:(n + 1) * 256])

    def transpose_rec(l, j, n):
        wt[l, n, rows(j * 256, 256), :] = w[l, 1, j, pl.ds(n * 256, 256), :].T

    def step_dots(l, t, h):
        zin = [gt[l, k, rows(t * B, B), :] for k in range(4)]
        prod = [None] * 8
        for k in (0, 2, 1, 3):
            for n in range(2):
                prod[2 * k + n] = dot(h, w[l, 1, 2 * k + n])
        return zin, prod

    def step_gates(l, t, zp, c):
        zin, prod = zp
        r0, r1_ = rows(t * B, B), rows((t + 1) * B, B)
        hs, cs = [], []
        for n in range(2):
            m = slice(n * 256, (n + 1) * 256)
            z = [zin[k][:, m] + prod[2 * k + n] for k in range(4)]
            i, g, f, o = sigmoid(z[0]), jnp.tanh(z[2]), sigmoid(z[1]), sigmoid(z[3])
            cn = f * c[:, m] + i * g
            th = jnp.tanh(cn)
            hn = (o * th).astype(BF16)
            for k, v in enumerate((i, f, g, o)):
                gt[l, k, r0, m] = v
            cb[l, r1_, m] = cn
            tc[l, r0, m] = th
            hb[l + 1, r1_, m] = hn
            hs.append(hn)
            cs.append(cn)
        return jnp.concatenate(hs, axis=1), jnp.concatenate(cs, axis=1)

    zero_state = (jnp.zeros((B, H), BF16), jnp.zeros((B, H), F32))
    for n in range(8):
        in_block(0, 0, n)
    for n in range(8):
        in_block(0, 2, n, 256)
    wait_w(0, 1)
    h0, c0 = zero_state
    for q in range(4):
        zp = step_dots(0, q, h0)
        in_block(0, 1, 2 * q)
        in_block(0, 1, 2 * q + 1)
        transpose_rec(0, q // 2, q % 2)
        h0, c0 = step_gates(0, q, zp, c0)
    wait_w(1, 0)
    wait_w(1, 1)

    def both(s, carry):
        h0, c0, h1, c1 = carry
        t0, t1 = 4 * s + 4, 4 * s
        a = step_dots(0, t0, h0)
        for n in range(8):
            in_block(1, s, n)
        h0, c0 = step_gates(0, t0, a, c0)
        for q in range(4):
            if q < 3:
                a = step_dots(0, t0 + q + 1, h0)
            b = step_dots(1, t1 + q, h1)
            if q < 3:
                h0, c0 = step_gates(0, t0 + q + 1, a, c0)
            transpose_rec(0, 2 * s + 2 + q // 2, q % 2)
            transpose_rec(1, 2 * s + q // 2, q % 2)
            h1, c1 = step_gates(1, t1 + q, b, c1)
        return h0, c0, h1, c1

    h0, c0, h1, c1 = lax.fori_loop(0, 3, both, (h0, c0) + zero_state)
    for n in range(8):
        in_block(1, 3, n)
    for q in range(4):
        zp = step_dots(1, 12 + q, h1)
        transpose_rec(1, 6 + q // 2, q % 2)
        h1, c1 = step_gates(1, 12 + q, zp, c1)

    pltpu.make_async_copy(dyv, dyv, lsem.at[1]).wait()
    dbacc[...] = jnp.zeros_like(dbacc)

    def bwd_layer(l, e_of, halfway=None):
        def body(s, carry):
            r, dc_next = carry
            t = T - 1 - s
            r0 = rows(t * B, B)
            i, f, g, o = [gt[l, k, r0, :] for k in range(4)]
            th, c_prev = tc[l, r0, :], cb[l, r0, :]
            dh = e_of(t) + r
            dc = dc_next + dh * o * (1.0 - th * th)
            dzs = (dc * g * i * (1.0 - i), dc * c_prev * f * (1.0 - f), dc * i * (1.0 - g * g), dh * th * o * (1.0 - o))
            acc = None
            for k in ORDER:
                d = dzs[k]
                dbacc[l, :, k * H:(k + 1) * H] += d[0:8] + d[8:16] + d[16:24] + d[24:32]
                d16 = d.astype(BF16)
                for n in range(2):
                    dz[l, 2 * k + n, r0, :] = d16[:, n * 256:(n + 1) * 256]
                p = [dot(d16, wt[l, n, pl.ds(k * H, H), :]) for n in range(2)]
                acc = p if acc is None else [a + b for a, b in zip(acc, p)]
            return jnp.concatenate(acc, axis=1), dc * f

        zero = jnp.zeros((B, H), F32)
        carry = (zero, zero)
        if halfway is None:
            lax.fori_loop(0, T, body, carry)
        else:
            carry = lax.fori_loop(0, T // 2, body, carry)
            halfway()
            lax.fori_loop(T // 2, T, body, carry)

    def dx_of(l, put):
        acc = None
        for m in range(2):
            rr = pl.ds(m * 256, 256)
            acc = None
            for j in range(8):
                p = dot_nt(dz[l, j, rr, :], w[l, 0, j])
                acc = p if acc is None else acc + p
            put(m, acc)

    def block_row(who, q, grp):
        b1 = bits[q][0]
        part = 1 - b1 if grp == 0 else b1
        return who * H + q * 256 + part * 128

    def cols(half):
        return pl.ds(pl.multiple_of(half * 1024, 1024), 1024)

    def half_of(q, h):
        b2 = bits[q][1]
        return 1 - b2 if h == 0 else b2

    def lhs_of(l, who, q, grp):
        r0 = block_row(who, q, grp)
        return hb[l + who, rows(B * (1 - who), R, B), rows(r0 - who * H, 128, 128)].T

    def dw_block(l, who, q, grp, h):
        lt = lhs_of(l, who, q, grp)
        half = half_of(q, h)
        for n in range(4):
            dwb[l, rows(block_row(who, q, grp), 128), pl.ds(pl.multiple_of(half * 1024 + n * 256, 256), 256)] = (
                dot(lt, dz[l, 4 * half + n]).astype(BF16))

    def cp_rp(l, q, grp, h):
        rr, cc = rows(block_row(1 - core, q, grp), 128), cols(half_of(q, h))
        return remote(dwb.at[l, rr, cc], rp.at[l, q, grp, h], s_rp, v_rp.at[l, q, grp, h], partner)

    def add_rp(l, q, grp, h):
        r0, cc = block_row(core, q, grp), cols(half_of(q, h))

        @pl.loop(0, 4)
        def _(i):
            rr = rows(r0 + i * 32, 32)
            dwb[l, rr, cc] = (dwb[l, rr, cc].astype(F32) + rp[l, q, grp, h, rows(i * 32, 32), :].astype(F32)).astype(BF16)

    def place(q, grp, h, i):
        return rows(block_row(core, q, grp) + C * i, C), cols(half_of(q, h))

    def cp_1(l, q, h, i):
        rr, cc = place(q, 0, h, i)
        return remote(dwb.at[l, rr, cc], r1.at[l, q, h, i], s_1, v_1.at[l, q, h, i], nbr[q][0])

    def cp_2(l, q, i):
        rr, cc = place(q, 1, 0, i)
        return remote(dwb.at[l, rr, cc], r2.at[l, q, i], s_2, v_2.at[l, q, i], nbr[q][1])

    def fin(q, k, i):
        b1, b2 = bits[q]
        c1 = b1 if k in (0, 1) else 1 - b1
        c2 = b2 if k in (0, 2) else 1 - b2
        return rows(core * H + q * 256 + c1 * 128 + C * i, C), cols(c2)

    def cp_a(l, q, k, i):
        rr, cc = fin(q, 1 if k == 2 else 0, i)
        return remote(res.at[l, rr, cc], res.at[l, rr, cc], s_a, v_a.at[l, q, k, i], nbr[q][1 if k == 0 else 0])

    def cp_p(l, q, k, i):
        rr, cc = fin(q, k, i)
        return remote(res.at[l, rr, cc], res.at[l, rr, cc], s_p, v_p, partner)

    QI = [(q, i) for i in range(2) for q in range(2)]

    def dw_pair(l, who, grp, h):
        for q in range(2):
            dw_block(l, who, q, grp, h)
            if who is not core:
                cp_rp(l, q, grp, h).start()

    def take_rp(l, grp, h):
        for q in range(2):
            cp_rp(l, q, grp, h).wait_recv()
            add_rp(l, q, grp, h)
            if grp == 0:
                for i in range(2):
                    cp_1(l, q, h, i).start()

    def grads_send(l):
        other = 1 - core
        dw_pair(l, other, 0, 0)
        dw_pair(l, core, 0, 0)
        dw_pair(l, other, 0, 1)
        take_rp(l, 0, 0)
        dw_pair(l, core, 0, 1)
        dw_pair(l, other, 1, 0)
        take_rp(l, 0, 1)
        dw_pair(l, core, 1, 0)
        dw_pair(l, other, 1, 1)
        dw_pair(l, core, 1, 1)

    def recv_1(l, h):
        if h == 0:
            take_rp(l, 1, 0)
            take_rp(l, 1, 1)
        for q, i in QI:
            cp_1(l, q, h, i).wait_recv()
            rr, cc = place(q, 1, h, i)
            dwb[l, rr, cc] = (dwb[l, rr, cc].astype(F32) + r1[l, q, h, i].astype(F32)).astype(BF16)
            if h == 0:
                cp_2(l, q, i).start()

    def recv_2(l):
        for q, i in QI:
            cp_2(l, q, i).wait_recv()
            rr, cc = fin(q, 0, i)
            res[l, rr, cc] = (dwb[l, rr, cc].astype(F32) + r2[l, q, i].astype(F32)).astype(BF16)
            cp_a(l, q, 0, i).start()
            cp_p(l, q, 0, i).start()

    def send_a1(l):
        for q, i in QI:
            cp_a(l, q, 1, i).start()

    def recv_a1(l):
        for q, i in QI:
            cp_a(l, q, 0, i).wait_recv()
            cp_a(l, q, 2, i).start()
            cp_p(l, q, 1, i).start()

    def recv_a2(l, k):
        for q, i in QI:
            cp_a(l, q, k, i).wait_recv()
            cp_p(l, q, k + 1, i).start()

    bwd_layer(1, lambda t: jnp.concatenate([dyv[k, pl.ds(t, B, stride=T), :] for k in range(4)], axis=1))
    pl.semaphore_wait(barrier, 7)
    grads_send(1)

    def put_e(m, v):
        eb[pl.ds(m * 256, 256), :] = v
    dx_of(1, put_e)
    bwd_layer(0, lambda t: eb[rows(t * B, B), :], lambda: recv_1(1, 0))
    grads_send(0)

    for l in range(2):
        for j in range(8):
            dbs[8 * l + j:8 * l + j + 1, :] = jnp.sum(dbacc[l, :, j * 256:(j + 1) * 256], axis=0, keepdims=True)
    dbb[...] = dbs[...].astype(BF16)
    me = rep * 4 + dat
    cps = [remote(dbb, dbr.at[d - 1], s_db, v_db, dev) for d, dev in enumerate(others, 1)]
    for c in cps:
        c.start()

    def put_dx(m, v):
        for s in range(8):
            for k in range(4):
                dxo[k, pl.ds(8 * m + s, B, stride=T), :] = v[s * B:(s + 1) * B, k * 128:(k + 1) * 128]

    recv_1(1, 1)
    recv_2(1)
    dx_of(0, put_dx)
    recv_1(0, 0)
    send_a1(1)
    recv_1(0, 1)
    recv_a1(1)
    recv_2(0)
    send_a1(0)
    recv_a2(1, 1)
    recv_a2(1, 2)
    remote(dbr, dbr, s_db, v_db, partner).wait_recv()
    tot = dbb[...].astype(F32)
    for d in range(7):
        tot += dbr[d].astype(F32)
    dbo[...] = tot
    recv_a1(0)
    recv_a2(0, 1)
    recv_a2(0, 2)
    half_w = dwb.at[:, pl.ds(0, H)]
    remote(half_w, half_w, s_rp, v_p, partner).wait_send()
    quarter = dwb.at[:, pl.ds(0, 256)]
    remote(quarter, quarter, s_1, v_p, partner).wait_send()
    eighth = dwb.at[:, pl.ds(0, 128)]
    remote(eighth, eighth, s_2, v_p, partner).wait_send()
    part = dwb.at[:, pl.ds(0, 384)]
    remote(part, part, s_a, v_p, partner).wait_send()
    mine = res.at[:, rows(core * H, H)]
    theirs = res.at[:, rows((1 - core) * H, H)]
    remote(mine, theirs, s_p, v_p, partner).wait()
    remote(dbr, dbr, s_db, v_db, partner).wait_send()


def out_kernel(res, dbo, dxo, dw_ref, db_ref, dx_ref, buf, dbv, sem, xsem):
    cx = [pltpu.make_async_copy(dxo.at[k], dx_ref.at[:, pl.ds(k * 128, 128)], xsem.at[k]) for k in range(4)]
    for l in range(2):
        for j in range(8):
            dbv[l:l + 1, j * 256:(j + 1) * 256] = dbo[8 * l + j:8 * l + j + 1, :]
    cx.append(pltpu.make_async_copy(dbv, db_ref, xsem.at[4]))
    for c in cx:
        c.start()
    n = 64

    def cp(s):
        return pltpu.make_async_copy(buf.at[s], dw_ref.at[s // 16, rows(lax.rem(s, 16) * n, n)], sem)

    @pl.loop(0, 32)
    def _(s):
        buf[s] = res[s // 16, rows(lax.rem(s, 16) * n, n), :].astype(F32)
        cp(s).start()

    pltpu.make_async_copy(buf, buf, sem).wait()
    for c in cx:
        c.wait()


def solution(mesh):
    vm = pl.BlockSpec(memory_space=pltpu.VMEM)
    hbm = pl.BlockSpec(memory_space=pl.ANY)
    dma = pltpu.SemaphoreType.DMA

    def local_step(x, dy, w, b):
        scratch = [
            pltpu.VMEM((2, G), F32),
            pltpu.VMEM((4, R, 128), BF16), pltpu.VMEM((4, B * PAD, 128), F32), pltpu.VMEM((4, R, 128), F32),
            pltpu.VMEM((2, 2, 8, H, 256), BF16), pltpu.VMEM((2, 2, G, 256), BF16), pltpu.VMEM((3, R + B, H), BF16),
            pltpu.VMEM((2, 4, R, H), F32), pltpu.VMEM((2, R + B, H), F32), pltpu.VMEM((2, R, H), F32),
            pltpu.VMEM((2, 8, R, 256), BF16), pltpu.VMEM((R, H), F32), pltpu.VMEM((2, 8, G), F32),
            pltpu.VMEM((16, 256), F32), pltpu.VMEM((16, 256), BF16), pltpu.VMEM((7, 16, 256), BF16),
            pltpu.VMEM((2, 2 * H, G), BF16), pltpu.VMEM((2, 2, 2, 2, 128, 1024), BF16),
            pltpu.VMEM((2, 2, 2, 2, C, 1024), BF16), pltpu.VMEM((2, 2, 2, C, 1024), BF16),
            dma((7,)), dma, dma((2, 2, 2, 2)), dma, dma((2, 2, 2, 2)), dma, dma((2, 2, 2)),
            dma, dma((2, 2, 3, 2)), dma, dma, dma, dma,
        ]
        res, dbo, dxo = pl.pallas_call(
            step_kernel,
            out_shape=(pltpu.VMEM((2, 2 * H, G), BF16), pltpu.VMEM((16, 256), F32), pltpu.VMEM((4, R, 128), F32)),
            in_specs=[hbm, hbm, hbm, hbm], out_specs=(vm, vm, vm), scratch_shapes=scratch,
            compiler_params=pltpu.CompilerParams(collective_id=0, has_side_effects=True, vmem_limit_bytes=VMEM_LIMIT),
        )(x.reshape(R, H), dy.reshape(R, H), w, b)
        dw, db, dx = pl.pallas_call(
            out_kernel,
            out_shape=(jax.ShapeDtypeStruct((2, 2 * H, G), F32), jax.ShapeDtypeStruct((2, G), F32),
                       jax.ShapeDtypeStruct((R, H), F32)),
            in_specs=[vm, vm, vm], out_specs=(hbm, hbm, hbm),
            scratch_shapes=[pltpu.VMEM((32, 64, G), F32), pltpu.VMEM((2, G), F32), dma, dma((5,))],
            compiler_params=pltpu.CompilerParams(vmem_limit_bytes=32 * 1024 * 1024),
        )(res, dbo, dxo)
        return dw, db, dx.reshape(B, T, H)

    rows_spec = P(("replica", "data"))
    return jax.shard_map(local_step, mesh=mesh, in_specs=(rows_spec, rows_spec, P(), P()),
                         out_specs=(P(), P(), rows_spec), check_vma=False)
```

time: 126 us -> 108 us (0.86)
  Pallas kernels: 120 us -> 107 us
  local copies, waits for them, and re-layouts: 5.32 us -> 0 us
    pallas_call x1, Pallas kernels: 113 us -> 101 us  [local_step(): pl.pallas_call(step_kernel, out_shape=(pltpu.VMEM((2, 2 * H, G), BF16), p...]
    unnamed x6 -> x0, local copies, waits for them, and re-layouts: 5.32 us -> none
where the time goes in v2:
time: 108 us
  Pallas kernels  107 us (99%)
    pallas_call x1, Pallas kernels, local_step(): pl.pallas_call(step_kernel, out_shape=(pltpu.VMEM((2, 2 * H, G), BF16), p...  101 us
    pallas_call x1, Pallas kernels, local_step(): pl.pallas_call(out_kernel, out_shape=(jax.ShapeDtypeStruct((2, 2 * H, G),...  6.17 us

profile of v2, /device:TPU:0, one launch (start us, length us, event | category | flops | bytes accessed | tf_op | source)
XLA Modules:
  0.0 108.0 jit_solution(14404287675290414430)
XLA Ops:
  0.6 101.0 %shard_map.67 = (bf16[2,1024,2048]{2,1,0:T(8,128)(2,1)S(1)}, f32[16,256]{1,0:T(8,128)S(1)}, f32[4,512,128]{2,1,0:T(8,128)S(1)}) custom-call(bf16[512,512]{1,0:T(8,128)(2,1)} %bitcast.4, f32[512,512]{1,0:T(8,128)} %bitcast.3, bf16[2,1024,2048]{2,1,0:T(8,128)(2,1)} %w_hbm.1, f32[2,2048]{1,0:T(2,128)} %b_hbm.1), custom_call_target="tpu_custom_call" | custom-call | tf_op jit(solution)/shard_map/pallas_call | solution.py:425
  101.6 6.2 %shard_map.68 = (f32[2,1024,2048]{2,1,0:T(8,128)}, f32[2,2048]{1,0:T(2,128)}, f32[512,512]{1,0:T(8,128)}) custom-call(bf16[2,1024,2048]{2,1,0:T(8,128)(2,1)S(1)} %get-tuple-element.9.res, f32[16,256]{1,0:T(8,128)S(1)} %get-tuple-element.10.dbo, f32[4,512,128]{2,1,0:T(8,128)S(1)} %get-tuple-element.11.dxo), custom_call_target="tpu_custom_call" | custom-call | tf_op jit(solution)/shard_map/pallas_call | solution.py:431

commit v3 on v2

--- a/solution.py
+++ b/solution.py
@@ -11,6 +11,7 @@
 G, R = 4 * H, T * B
 ORDER = (0, 1, 2, 3)
 PAD = 24
+CUT = (5, 13)
 VMEM_LIMIT = 54 * 1024 * 1024
 C = 64
 
@@ -33,7 +34,9 @@
 
 def step_kernel(x_hbm, dy_hbm, w_hbm, b_hbm, res, dbo, dxo,
                 b_ref, xv, xf, dyv, w, wt, hb, gt, cb, tc, dz, eb, dbacc, dbs, dbb, dbr, dwb, rp, r1, r2,
-                lsem, s_rp, v_rp, s_1, v_1, s_2, v_2, s_a, v_a, s_p, v_p, s_db, v_db):
+                hx, zx, ub, rph, r1h, r2u, r2h,
+                lsem, s_rp, v_rp, s_1, v_1, s_2, v_2, s_a, v_a, s_p, v_p, s_db, v_db,
+                s_h, v_h, s_z, v_z, s_rph, v_rph, s_1h, v_1h, s_2x, v_2x, s_ax, v_ax, s_px, v_px):
     rep = lax.axis_index("replica")
     dat = lax.axis_index("data")
     mx, core = dat // 2, dat % 2
@@ -132,9 +135,30 @@
     wait_w(1, 0)
     wait_w(1, 1)
 
+    def pick(a, b):
+        return a + core * (b - a)
+
+    u_b1, u_b2 = pick(mx, rep), pick(rep, mx)
+    u_n1 = (pick(rep, 1 - rep), pick(lax.rem(dat + 2, 4), dat))
+    u_n2 = (pick(1 - rep, rep), pick(dat, lax.rem(dat + 2, 4)))
+    x_core0, y_core1 = (rep, 2 * (1 - mx)), (1 - rep, 2 * mx + 1)
+    dests = ((partner, 0, pick(4 + 2 * rep, 2 * mx)), (x_core0, 1 + core, 2 * (1 - mx)), (y_core1, 1 + core, 4 + 2 * (1 - rep)))
+    u_col = pick(2 * mx, 4 + 2 * rep)
+
+    def send_h(s):
+        for dev, slot, _ in dests:
+            remote(hb.at[1, rows(B + s * 128, 128)], hx.at[slot, rows(s * 128, 128)], s_h, v_h.at[slot], dev).start()
+
+    def send_z(r0, n):
+        for dev, slot, c0 in dests:
+            remote(dz.at[1, pl.ds(c0, 2), rows(r0, n)], zx.at[slot, :, rows(r0, n)], s_z, v_z.at[slot], dev).start()
+
+    pl.semaphore_wait(barrier, 7)
+
     def both(s, carry):
         h0, c0, h1, c1 = carry
         t0, t1 = 4 * s + 4, 4 * s
+        send_h(s)
         a = step_dots(0, t0, h0)
         for n in range(8):
             in_block(1, s, n)
@@ -151,6 +175,7 @@
         return h0, c0, h1, c1
 
     h0, c0, h1, c1 = lax.fori_loop(0, 3, both, (h0, c0) + zero_state)
+    send_h(3)
     for n in range(8):
         in_block(1, 3, n)
     for q in range(4):
@@ -161,7 +186,7 @@
     pltpu.make_async_copy(dyv, dyv, lsem.at[1]).wait()
     dbacc[...] = jnp.zeros_like(dbacc)
 
-    def bwd_layer(l, e_of, halfway=None):
+    def bwd_layer(l, e_of, halfway=None, every_2=None):
         def body(s, carry):
             r, dc_next = carry
             t = T - 1 - s
@@ -184,12 +209,19 @@
 
         zero = jnp.zeros((B, H), F32)
         carry = (zero, zero)
-        if halfway is None:
-            lax.fori_loop(0, T, body, carry)
+        if every_2 is not None:
+            def two(u, carry):
+                carry = body(2 * u, carry)
+                carry = body(2 * u + 1, carry)
+                every_2((T - 2 - 2 * u) * B)
+                return carry
+            lax.fori_loop(0, T // 2, two, carry)
         else:
-            carry = lax.fori_loop(0, T // 2, body, carry)
-            halfway()
-            lax.fori_loop(T // 2, T, body, carry)
+            carry = lax.fori_loop(0, CUT[0], body, carry)
+            halfway(0)
+            carry = lax.fori_loop(CUT[0], CUT[1], body, carry)
+            halfway(1)
+            lax.fori_loop(CUT[1], T, body, carry)
 
     def dx_of(l, put):
         acc = None
@@ -226,7 +258,7 @@
 
     def cp_rp(l, q, grp, h):
         rr, cc = rows(block_row(1 - core, q, grp), 128), cols(half_of(q, h))
-        return remote(dwb.at[l, rr, cc], rp.at[l, q, grp, h], s_rp, v_rp.at[l, q, grp, h], partner)
+        return remote(dwb.at[l, rr, cc], rp.at[q, grp, h], s_rp, v_rp.at[q, grp, h], partner)
 
     def add_rp(l, q, grp, h):
         r0, cc = block_row(core, q, grp), cols(half_of(q, h))
@@ -234,18 +266,18 @@
         @pl.loop(0, 4)
         def _(i):
             rr = rows(r0 + i * 32, 32)
-            dwb[l, rr, cc] = (dwb[l, rr, cc].astype(F32) + rp[l, q, grp, h, rows(i * 32, 32), :].astype(F32)).astype(BF16)
+            dwb[l, rr, cc] = (dwb[l, rr, cc].astype(F32) + rp[q, grp, h, rows(i * 32, 32), :].astype(F32)).astype(BF16)
 
     def place(q, grp, h, i):
         return rows(block_row(core, q, grp) + C * i, C), cols(half_of(q, h))
 
     def cp_1(l, q, h, i):
         rr, cc = place(q, 0, h, i)
-        return remote(dwb.at[l, rr, cc], r1.at[l, q, h, i], s_1, v_1.at[l, q, h, i], nbr[q][0])
+        return remote(dwb.at[l, rr, cc], r1.at[q, h, i], s_1, v_1.at[q, h, i], nbr[q][0])
 
     def cp_2(l, q, i):
         rr, cc = place(q, 1, 0, i)
-        return remote(dwb.at[l, rr, cc], r2.at[l, q, i], s_2, v_2.at[l, q, i], nbr[q][1])
+        return remote(dwb.at[l, rr, cc], r2.at[q, i], s_2, v_2.at[q, i], nbr[q][1])
 
     def fin(q, k, i):
         b1, b2 = bits[q]
@@ -255,7 +287,7 @@
 
     def cp_a(l, q, k, i):
         rr, cc = fin(q, 1 if k == 2 else 0, i)
-        return remote(res.at[l, rr, cc], res.at[l, rr, cc], s_a, v_a.at[l, q, k, i], nbr[q][1 if k == 0 else 0])
+        return remote(res.at[l, rr, cc], res.at[l, rr, cc], s_a, v_a.at[q, k, i], nbr[q][1 if k == 0 else 0])
 
     def cp_p(l, q, k, i):
         rr, cc = fin(q, k, i)
@@ -297,7 +329,7 @@
         for q, i in QI:
             cp_1(l, q, h, i).wait_recv()
             rr, cc = place(q, 1, h, i)
-            dwb[l, rr, cc] = (dwb[l, rr, cc].astype(F32) + r1[l, q, h, i].astype(F32)).astype(BF16)
+            dwb[l, rr, cc] = (dwb[l, rr, cc].astype(F32) + r1[q, h, i].astype(F32)).astype(BF16)
             if h == 0:
                 cp_2(l, q, i).start()
 
@@ -305,7 +337,7 @@
         for q, i in QI:
             cp_2(l, q, i).wait_recv()
             rr, cc = fin(q, 0, i)
-            res[l, rr, cc] = (dwb[l, rr, cc].astype(F32) + r2[l, q, i].astype(F32)).astype(BF16)
+            res[l, rr, cc] = (dwb[l, rr, cc].astype(F32) + r2[q, i].astype(F32)).astype(BF16)
             cp_a(l, q, 0, i).start()
             cp_p(l, q, 0, i).start()
 
@@ -324,14 +356,145 @@
             cp_a(l, q, k, i).wait_recv()
             cp_p(l, q, k + 1, i).start()
 
-    bwd_layer(1, lambda t: jnp.concatenate([dyv[k, pl.ds(t, B, stride=T), :] for k in range(4)], axis=1))
-    pl.semaphore_wait(barrier, 7)
-    grads_send(1)
+    def h_row(who, q):
+        return H + who * 256 + q * 128
+
+    def dwh_block(who, q, grp):
+        lt = hb[2, pl.ds(0, R), rows(h_row(who, q) - H, 128, 128)].T
+        half = 1 - bits[q][0] if grp == 0 else bits[q][0]
+        for n in range(4):
+            dwb[1, rows(h_row(who, q), 128), pl.ds(pl.multiple_of(half * 1024 + n * 256, 256), 256)] = (
+                dot(lt, dz[1, 4 * half + n]).astype(BF16))
+
+    def cp_rph(q, grp):
+        half = 1 - bits[q][0] if grp == 0 else bits[q][0]
+        return remote(dwb.at[1, rows(h_row(1 - core, q), 128), cols(half)], rph.at[q, grp], s_rph, v_rph.at[q, grp], partner)
+
+    def quarter(q, grp, h):
+        half = 1 - bits[q][0] if grp == 0 else bits[q][0]
+        return pl.ds(pl.multiple_of(half * 1024 + 512 * half_of(q, h), 512), 512)
+
+    def cp_1h(q, h):
+        return remote(dwb.at[1, rows(h_row(core, q), 128), quarter(q, 0, h)], r1h.at[q, h], s_1h, v_1h.at[q, h], nbr[q][0])
+
+    def take_rph(grp):
+        for q in range(2):
+            cp_rph(q, grp).wait_recv()
+            r0, cc = h_row(core, q), cols(1 - bits[q][0] if grp == 0 else bits[q][0])
+
+            @pl.loop(0, 4)
+            def _(i):
+                rr = rows(r0 + i * 32, 32)
+                dwb[1, rr, cc] = (dwb[1, rr, cc].astype(F32) + rph[q, grp, rows(i * 32, 32), :].astype(F32)).astype(BF16)
+            if grp == 0:
+                for h in range(2):
+                    cp_1h(q, h).start()
+
+    def grads_send_1():
+        for grp in range(2):
+            for q in range(2):
+                dwh_block(1 - core, q, grp)
+                cp_rph(q, grp).start()
+            for q in range(2):
+                dwh_block(core, q, grp)
+            if grp == 0:
+                take_rph(0)
+
+    def sum_u():
+        for i in range(3):
+            remote(hx.at[i], hx.at[i], s_h, v_h.at[i], partner).wait_recv()
+            remote(zx.at[i], zx.at[i], s_z, v_z.at[i], partner).wait_recv()
+        for m in range(4):
+            f0 = pl.ds(m * 128, 128)
+            lts = [hb[1, pl.ds(B, R), f0].T] + [hx[i, :, f0].T for i in range(3)]
+            for n in range(2):
+                zs = [dz[1, u_col + n]] + [zx[i, n] for i in range(3)]
+                acc = None
+                for lt, z in zip(lts, zs):
+                    p = dot(lt, z).astype(BF16).astype(F32)
+                    acc = p if acc is None else acc + p
+                ub[f0, n * 256:(n + 1) * 256] = acc.astype(BF16)
+
+    def item_nbr(j):
+        return (u_n1, u_n2) if j < 2 else nbr[j - 2]
+
+    def item_fin(j, k):
+        b1, b2 = (u_b1, u_b2) if j < 2 else bits[j - 2]
+        c1 = b1 if k in (0, 1) else 1 - b1
+        c2 = b2 if k in (0, 2) else 1 - b2
+        if j < 2:
+            return rows(256 * c2 + 128 * j, 128), pl.ds(pl.multiple_of(core * 1024 + 512 * c1, 512), 512)
+        return rows(h_row(core, j - 2), 128), pl.ds(pl.multiple_of(1024 * c1 + 512 * c2, 512), 512)
+
+    def cp_2x(j):
+        if j < 2:
+            src, dst = ub.at[rows(256 * (1 - u_b2) + 128 * j, 128)], r2u.at[j]
+        else:
+            src, dst = dwb.at[1, rows(h_row(core, j - 2), 128), quarter(j - 2, 1, 0)], r2h.at[j - 2]
+        return remote(src, dst, s_2x, v_2x.at[j], item_nbr(j)[1])
+
+    def cp_ax(j, k):
+        rr, cc = item_fin(j, 1 if k == 2 else 0)
+        return remote(res.at[1, rr, cc], res.at[1, rr, cc], s_ax, v_ax.at[j, k], item_nbr(j)[1 if k == 0 else 0])
+
+    def cp_px(j, k):
+        rr, cc = item_fin(j, k)
+        return remote(res.at[1, rr, cc], res.at[1, rr, cc], s_px, v_px, partner)
+
+    JS = (2, 3, 0, 1)
+
+    def recv_1h(h):
+        if h == 0:
+            take_rph(1)
+        for q in range(2):
+            cp_1h(q, h).wait_recv()
+            rr, cc = rows(h_row(core, q), 128), quarter(q, 1, h)
+            dwb[1, rr, cc] = (dwb[1, rr, cc].astype(F32) + r1h[q, h].astype(F32)).astype(BF16)
+            if h == 0:
+                cp_2x(2 + q).start()
+
+    def recv_2x():
+        for j in JS:
+            cp_2x(j).wait_recv()
+            rr, cc = item_fin(j, 0)
+            if j < 2:
+                mine, got = ub[rows(256 * u_b2 + 128 * j, 128), :], r2u[j]
+            else:
+                mine, got = dwb[1, rr, cc], r2h[j - 2]
+            res[1, rr, cc] = (mine.astype(F32) + got.astype(F32)).astype(BF16)
+            cp_ax(j, 0).start()
+            cp_px(j, 0).start()
+
+    def send_a1x():
+        for j in JS:
+            cp_ax(j, 1).start()
+
+    def recv_a1x():
+        for j in JS:
+            cp_ax(j, 0).wait_recv()
+            cp_ax(j, 2).start()
+            cp_px(j, 1).start()
+
+    def recv_a2x(k):
+        for j in JS:
+            cp_ax(j, k).wait_recv()
+            cp_px(j, k + 1).start()
+
+    def between(part):
+        if part == 0:
+            sum_u()
+            for j in range(2):
+                cp_2x(j).start()
+        else:
+            recv_1h(0)
+
+    bwd_layer(1, lambda t: jnp.concatenate([dyv[k, pl.ds(t, B, stride=T), :] for k in range(4)], axis=1), every_2=lambda r0: send_z(r0, 2 * B))
+    grads_send_1()
 
     def put_e(m, v):
         eb[pl.ds(m * 256, 256), :] = v
     dx_of(1, put_e)
-    bwd_layer(0, lambda t: eb[rows(t * B, B), :], lambda: recv_1(1, 0))
+    bwd_layer(0, lambda t: eb[rows(t * B, B), :], between)
     grads_send(0)
 
     for l in range(2):
@@ -348,17 +511,17 @@
             for k in range(4):
                 dxo[k, pl.ds(8 * m + s, B, stride=T), :] = v[s * B:(s + 1) * B, k * 128:(k + 1) * 128]
 
-    recv_1(1, 1)
-    recv_2(1)
+    recv_1h(1)
+    recv_2x()
     dx_of(0, put_dx)
     recv_1(0, 0)
-    send_a1(1)
+    send_a1x()
     recv_1(0, 1)
-    recv_a1(1)
+    recv_a1x()
     recv_2(0)
     send_a1(0)
-    recv_a2(1, 1)
-    recv_a2(1, 2)
+    recv_a2x(1)
+    recv_a2x(2)
     remote(dbr, dbr, s_db, v_db, partner).wait_recv()
     tot = dbb[...].astype(F32)
     for d in range(7):
@@ -367,17 +530,14 @@
     recv_a1(0)
     recv_a2(0, 1)
     recv_a2(0, 2)
-    half_w = dwb.at[:, pl.ds(0, H)]
-    remote(half_w, half_w, s_rp, v_p, partner).wait_send()
-    quarter = dwb.at[:, pl.ds(0, 256)]
-    remote(quarter, quarter, s_1, v_p, partner).wait_send()
-    eighth = dwb.at[:, pl.ds(0, 128)]
-    remote(eighth, eighth, s_2, v_p, partner).wait_send()
-    part = dwb.at[:, pl.ds(0, 384)]
-    remote(part, part, s_a, v_p, partner).wait_send()
-    mine = res.at[:, rows(core * H, H)]
-    theirs = res.at[:, rows((1 - core) * H, H)]
-    remote(mine, theirs, s_p, v_p, partner).wait()
+    for n, sem in ((512, s_rp), (256, s_1), (128, s_2), (384, s_a), (256, s_rph), (128, s_1h), (128, s_2x), (384, s_ax)):
+        part = dwb.at[0, pl.ds(0, n)]
+        remote(part, part, sem, v_p, partner).wait_send()
+    remote(hx, hx, s_h, v_p, partner).wait_send()
+    remote(zx, zx, s_z, v_p, partner).wait_send()
+    for l, snd, rcv in ((0, s_p, v_p), (1, s_px, v_px)):
+        half_w = res.at[l, pl.ds(0, H)]
+        remote(half_w, half_w, snd, rcv, partner).wait()
     remote(dbr, dbr, s_db, v_db, partner).wait_send()
 
 
@@ -417,10 +577,14 @@
             pltpu.VMEM((2, 4, R, H), F32), pltpu.VMEM((2, R + B, H), F32), pltpu.VMEM((2, R, H), F32),
             pltpu.VMEM((2, 8, R, 256), BF16), pltpu.VMEM((R, H), F32), pltpu.VMEM((2, 8, G), F32),
             pltpu.VMEM((16, 256), F32), pltpu.VMEM((16, 256), BF16), pltpu.VMEM((7, 16, 256), BF16),
-            pltpu.VMEM((2, 2 * H, G), BF16), pltpu.VMEM((2, 2, 2, 2, 128, 1024), BF16),
-            pltpu.VMEM((2, 2, 2, 2, C, 1024), BF16), pltpu.VMEM((2, 2, 2, C, 1024), BF16),
-            dma((7,)), dma, dma((2, 2, 2, 2)), dma, dma((2, 2, 2, 2)), dma, dma((2, 2, 2)),
-            dma, dma((2, 2, 3, 2)), dma, dma, dma, dma,
+            pltpu.VMEM((2, 2 * H, G), BF16), pltpu.VMEM((2, 2, 2, 128, 1024), BF16),
+            pltpu.VMEM((2, 2, 2, C, 1024), BF16), pltpu.VMEM((2, 2, C, 1024), BF16),
+            pltpu.VMEM((3, R, H), BF16), pltpu.VMEM((3, 2, R, 256), BF16), pltpu.VMEM((H, 512), BF16),
+            pltpu.VMEM((2, 2, 128, 1024), BF16), pltpu.VMEM((2, 2, 128, 512), BF16), pltpu.VMEM((2, 128, 512), BF16),
+            pltpu.VMEM((2, 128, 512), BF16),
+            dma((7,)), dma, dma((2, 2, 2)), dma, dma((2, 2, 2)), dma, dma((2, 2)),
+            dma, dma((2, 3, 2)), dma, dma, dma, dma,
+            dma, dma((3,)), dma, dma((3,)), dma, dma((2, 2)), dma, dma((2, 2)), dma, dma((4,)), dma, dma((4, 3)), dma, dma,
         ]
         res, dbo, dxo = pl.pallas_call(
             step_kernel,

time: 108 us -> 105 us (0.972)
  Pallas kernels: 107 us -> 104 us
    pallas_call x1, Pallas kernels: 101 us -> 98 us  [local_step(): pl.pallas_call(step_kernel, out_shape=(pltpu.VMEM((2, 2 * H, G), BF16), p...]
where the time goes in v3:
time: 105 us
  Pallas kernels  104 us (99%)
    pallas_call x1, Pallas kernels, local_step(): pl.pallas_call(step_kernel, out_shape=(pltpu.VMEM((2, 2 * H, G), BF16), p...  98 us
    pallas_call x1, Pallas kernels, local_step(): pl.pallas_call(out_kernel, out_shape=(jax.ShapeDtypeStruct((2, 2 * H, G),...  6.17 us

profile of v3, /device:TPU:0, one launch (start us, length us, event | category | flops | bytes accessed | tf_op | source)
XLA Modules:
  0.0 105.0 jit_solution(11170888421172479156)
XLA Ops:
  0.6 98.0 %shard_map.67 = (bf16[2,1024,2048]{2,1,0:T(8,128)(2,1)S(1)}, f32[16,256]{1,0:T(8,128)S(1)}, f32[4,512,128]{2,1,0:T(8,128)S(1)}) custom-call(bf16[512,512]{1,0:T(8,128)(2,1)} %bitcast.4, f32[512,512]{1,0:T(8,128)} %bitcast.3, bf16[2,1024,2048]{2,1,0:T(8,128)(2,1)} %w_hbm.1, f32[2,2048]{1,0:T(2,128)} %b_hbm.1), custom_call_target="tpu_custom_call" | custom-call | tf_op jit(solution)/shard_map/pallas_call | solution.py:589
  98.7 6.2 %shard_map.68 = (f32[2,1024,2048]{2,1,0:T(8,128)}, f32[2,2048]{1,0:T(2,128)}, f32[512,512]{1,0:T(8,128)}) custom-call(bf16[2,1024,2048]{2,1,0:T(8,128)(2,1)S(1)} %get-tuple-element.9.res, f32[16,256]{1,0:T(8,128)S(1)} %get-tuple-element.10.dbo, f32[4,512,128]{2,1,0:T(8,128)S(1)} %get-tuple-element.11.dxo), custom_call_target="tpu_custom_call" | custom-call | tf_op jit(solution)/shard_map/pallas_call | solution.py:595

commit v4 on v3

v4 whole, which is shorter than its diff:
```python
import jax
import jax.numpy as jnp
from jax import lax
from jax.experimental import pallas as pl
from jax.experimental.pallas import tpu as pltpu
from jax.sharding import PartitionSpec as P

F32, BF16 = jnp.float32, jnp.bfloat16
MESH = pl.DeviceIdType.MESH
T, B, H = 16, 32, 512
G, R = 4 * H, T * B
ORDER = (0, 1, 2, 3)
PAD = 24
MID = 2
CUT = (6, 13)
TWO, THREE, FOUR, EIGHT = range(2), range(3), range(4), range(8)
W = 256
BLK, QTR, HALF, SUB = 128, 512, 1024, 16
P2, P3 = (2, 2), (2, 2, 2)
VMEM_LIMIT = 54 * 1024 * 1024
C = 64


def flip(bit):
    return 1 - bit


def loop(n):
    return pl.loop(0, n)


def dot(a, b):
    return jnp.dot(a, b, preferred_element_type=F32)


def dot_nt(a, b):
    return lax.dot_general(a, b, (((1,), (1,)), ((), ())), preferred_element_type=F32)


def sigmoid(z):
    return 0.5 * jnp.tanh(0.5 * z) + 0.5


def rows(start, n, m=SUB):
    return pl.ds(start, n) if isinstance(start, int) else pl.ds(pl.multiple_of(start, m), n)


def step_kernel(x_hbm, dy_hbm, w_hbm, b_hbm, res, dbo, dxo,
                b_ref, xv, xf, dyv, w, wt, hb, gt, cb, tc, dz, eb, dbacc, dbs, dbb, dbr, dwb, rp, r1, r2,
                hx, zx, ub, rph, r1h, r2u, r2h,
                lsem, s_rp, v_rp, s_1, v_1, s_2, v_2, s_a, v_a, s_p, v_p, s_db, v_db,
                s_h, v_h, s_z, v_z, s_rph, v_rph, s_1h, v_1h, s_2x, v_2x, s_ax, v_ax, s_px, v_px):
    rep = lax.axis_index("replica")
    dat = lax.axis_index("data")
    mx, core = dat // 2, dat % 2
    partner = (rep, dat + 1 - 2 * core)
    x_nbr = (rep, lax.rem(dat + 2, 4))
    y_nbr = (flip(rep), dat)
    nbr = ((x_nbr, y_nbr), (y_nbr, x_nbr))
    bits = ((mx, rep), (rep, mx))

    def remote(src, dst, s, v, dev):
        return pltpu.make_async_remote_copy(src_ref=src, dst_ref=dst, send_sem=s, recv_sem=v,
                                            device_id=dev, device_id_type=MESH)

    others = [(lax.rem(rep + (d // 4), 2), lax.rem(dat + (d % 4), 4)) for d in range(1, 8)]
    barrier = pltpu.get_barrier_semaphore()

    ld_x = [pltpu.make_async_copy(x_hbm.at[:, pl.ds(k * BLK, BLK)], xv.at[k], lsem.at[0]) for k in FOUR]
    ld_dy = [pltpu.make_async_copy(dy_hbm.at[:, pl.ds(k * BLK, BLK)], dyv.at[k], lsem.at[1]) for k in FOUR]
    ld_w = [pltpu.make_async_copy(w_hbm.at[l, pl.ds(k * H, H), pl.ds(j * W, W)], w.at[l, k, j],
                                  lsem.at[2 + 2 * l + k])
            for l in TWO for k in TWO for j in EIGHT]
    ld_b = pltpu.make_async_copy(b_hbm, b_ref, lsem.at[6])
    for c in ld_x + [ld_b] + ld_w[:8]:
        c.start()
    for dev in others:
        pl.semaphore_signal(barrier, inc=1, device_id=dev, device_id_type=MESH)
    for l in TWO:
        hb[l + 1, pl.ds(0, B), :] = jnp.zeros((B, H), BF16)
        cb[l, pl.ds(0, B), :] = jnp.zeros((B, H), F32)
    pltpu.make_async_copy(xv, xv, lsem.at[0]).wait()
    for c in ld_w[8:SUB]:
        c.start()
    for i in range(B):
        xf[:, i * PAD:i * PAD + T, :] = xv[:, i * T:(i + 1) * T, :].astype(F32)

    @loop(T)
    def _(t):
        hb[0, rows((t + 1) * B, B), :] = jnp.concatenate(
            [xf[k, pl.ds(t, B, stride=PAD), :] for k in FOUR], axis=1).astype(BF16)
    for c in ld_w[SUB:] + ld_dy:
        c.start()

    def wait_w(l, k):
        pltpu.make_async_copy(w.at[l, k], w.at[l, k], lsem.at[2 + 2 * l + k]).wait()

    ld_b.wait()
    pltpu.make_async_copy(w.at[0, 0], w.at[0, 0], lsem.at[2]).wait()

    def in_block(l, s, n, m=BLK):
        r0 = rows(s * BLK, m)
        gt[l, n // 2, r0, W * (n % 2):W * (n % 2) + W] = (
            dot(hb[l, rows(B + s * BLK, m), :], w[l, 0, n]) + b_ref[l:l + 1, W * n:W * n + W])

    def transpose_rec(l, j, n):
        wt[l, n, rows(j * W, W), :] = w[l, 1, j, pl.ds(n * W, W), :].T

    def step_dots(l, t, h):
        zin = [gt[l, k, rows(t * B, B), :] for k in FOUR]
        prod = [None] * 8
        if h is None:
            return zin, prod
        for k in (0, 2, 1, 3):
            for n in TWO:
                prod[2 * k + n] = dot(h, w[l, 1, 2 * k + n])
        return zin, prod

    def step_gates(l, t, zp, c):
        zin, prod = zp
        r0, r1_ = rows(t * B, B), rows((t + 1) * B, B)
        hs, cs = [], []
        for n in TWO:
            m = slice(W * n, W * n + W)
            z = [zin[k][:, m] if prod[2 * k + n] is None else zin[k][:, m] + prod[2 * k + n] for k in FOUR]
            i, g, f, o = sigmoid(z[0]), jnp.tanh(z[2]), sigmoid(z[1]), sigmoid(z[3])
            cn = f * c[:, m] + i * g
            th = jnp.tanh(cn)
            hn = (o * th).astype(BF16)
            for k, v in enumerate((i, f, g, o)):
                gt[l, k, r0, m] = v
            cb[l, r1_, m] = cn
            tc[l, r0, m] = th
            hb[l + 1, r1_, m] = hn
            hs.append(hn)
            cs.append(cn)
        return jnp.concatenate(hs, axis=1), jnp.concatenate(cs, axis=1)

    zero_state = (jnp.zeros((B, H), BF16), jnp.zeros((B, H), F32))
    for n in EIGHT:
        in_block(0, 0, n)
    h0, c0 = None, zero_state[1]
    for q in FOUR:
        if q == 1:
            wait_w(0, 1)
        zp = step_dots(0, q, h0)
        if q == 0:
            for n in EIGHT:
                in_block(0, 2, n, 2 * BLK)
        in_block(0, 1, 2 * q)
        in_block(0, 1, 2 * q + 1)
        if q:
            transpose_rec(0, q // 2, q % 2)
        if q == 1:
            transpose_rec(0, 0, 0)
        h0, c0 = step_gates(0, q, zp, c0)
    wait_w(1, 0)
    wait_w(1, 1)

    def pick(a, b):
        return a + core * (b - a)

    u_b1, u_b2 = pick(mx, rep), pick(rep, mx)
    u_n1 = (pick(rep, flip(rep)), pick(lax.rem(dat + 2, 4), dat))
    u_n2 = (pick(flip(rep), rep), pick(dat, lax.rem(dat + 2, 4)))
    x_core0, y_core1 = (rep, 2 * (flip(mx))), (flip(rep), 2 * mx + 1)
    dests = ((partner, 0, pick(4 + 2 * rep, 2 * mx)), (x_core0, 1 + core, 2 * (flip(mx))), (y_core1, 1 + core, 4 + 2 * (flip(rep))))
    u_col = pick(2 * mx, 4 + 2 * rep)

    def send_h(r0, n):
        for dev, slot, _ in dests:
            remote(hb.at[1, rows(B + r0, n)], hx.at[slot, rows(r0, n)], s_h, v_h, dev).start()

    def send_z(r0, n):
        for dev, slot, c0 in dests:
            remote(dz.at[1, pl.ds(c0, 2), rows(r0, n)], zx.at[slot, :, rows(r0, n)], s_z, v_z, dev).start()

    pl.semaphore_wait(barrier, 7)

    def both(s, carry, last=False):
        h0, c0, h1, c1 = carry
        t0, t1 = 4 * s + 4, 4 * s
        send_h(s * BLK, BLK)
        a = step_dots(0, t0, h0)
        for n in EIGHT:
            in_block(1, s, n)
        h0, c0 = step_gates(0, t0, a, c0)
        for q in FOUR:
            if q < 3:
                a = step_dots(0, t0 + q + 1, h0)
            b = step_dots(1, t1 + q, h1)
            if q < 3:
                h0, c0 = step_gates(0, t0 + q + 1, a, c0)
            transpose_rec(0, 2 * s + 2 + q // 2, q % 2)
            transpose_rec(1, 2 * s + q // 2, q % 2)
            h1, c1 = step_gates(1, t1 + q, b, c1)
            if last and q == MID:
                send_h(6 * 2 * B, 2 * B)
        return h0, c0, h1, c1

    carry = both(0, (h0, c0, None, zero_state[1]))
    carry = both(1, carry)
    h0, c0, h1, c1 = both(2, carry, True)
    send_h(7 * 2 * B, 2 * B)
    for n in EIGHT:
        in_block(1, 3, n)
    for q in FOUR:
        zp = step_dots(1, 12 + q, h1)
        transpose_rec(1, 6 + q // 2, q % 2)
        h1, c1 = step_gates(1, 12 + q, zp, c1)

    pltpu.make_async_copy(dyv, dyv, lsem.at[1]).wait()
    dbacc[...] = jnp.zeros_like(dbacc)

    def bwd_layer(l, e_of, halfway=None, after=None):
        def body(s, carry):
            r, dc_next = carry
            t = T - 1 - s
            r0 = rows(t * B, B)
            i, f, g, o = [gt[l, k, r0, :] for k in FOUR]
            th, c_prev = tc[l, r0, :], cb[l, r0, :]
            dh = e_of(t) + r
            dc = dc_next + dh * o * (1.0 - th * th)
            dzs = (dc * g * i * (1.0 - i), dc * c_prev * f * (1.0 - f), dc * i * (1.0 - g * g), dh * th * o * (1.0 - o))
            acc = None
            for k in ORDER:
                d = dzs[k]
                dbacc[l, :, k * H:(k + 1) * H] += d[0:8] + d[8:SUB] + d[SUB:24] + d[24:32]
                d16 = d.astype(BF16)
                for n in TWO:
                    dz[l, 2 * k + n, r0, :] = d16[:, W * n:W * n + W]
                p = [dot(d16, wt[l, n, pl.ds(k * H, H), :]) for n in TWO]
                acc = p if acc is None else [a + b for a, b in zip(acc, p)]
            return jnp.concatenate(acc, axis=1), dc * f

        zero = jnp.zeros((B, H), F32)
        carry = (zero, zero)
        if after is not None:
            def step_and_send(s, carry):
                carry = body(s, carry)
                after((T - 1 - s) * B)
                return carry
            lax.fori_loop(0, T, step_and_send, carry)
        else:
            carry = lax.fori_loop(0, CUT[0], body, carry)
            halfway(0)
            carry = lax.fori_loop(CUT[0], CUT[1], body, carry)
            halfway(1)
            lax.fori_loop(CUT[1], T, body, carry)

    def dx_of(l, put):
        acc = None
        for m in TWO:
            rr = pl.ds(m * W, W)
            acc = None
            for j in EIGHT:
                p = dot_nt(dz[l, j, rr, :], w[l, 0, j])
                acc = p if acc is None else acc + p
            put(m, acc)

    def block_row(who, q, grp):
        b1 = bits[q][0]
        part = flip(b1) if grp == 0 else b1
        return who * H + q * W + part * BLK

    def cols(half):
        return pl.ds(pl.multiple_of(half * HALF, HALF), HALF)

    def half_of(q, h):
        b2 = bits[q][1]
        return flip(b2) if h == 0 else b2

    def lhs_of(l, who, q, grp):
        r0 = block_row(who, q, grp)
        return hb[l + who, rows(B * (flip(who)), R, B), rows(r0 - who * H, BLK, BLK)].T

    def dw_block(l, who, q, grp, h):
        lt = lhs_of(l, who, q, grp)
        half = half_of(q, h)
        for n in FOUR:
            dwb[l, rows(block_row(who, q, grp), BLK), pl.ds(pl.multiple_of(half * HALF + n * W, W), W)] = (
                dot(lt, dz[l, 4 * half + n]).astype(BF16))

    def cp_rp(l, q, grp, h):
        rr, cc = rows(block_row(flip(core), q, grp), BLK), cols(half_of(q, h))
        return remote(dwb.at[l, rr, cc], rp.at[q, grp, h], s_rp, v_rp.at[grp, h], partner)

    def add_rp(l, q, grp, h):
        r0, cc = block_row(core, q, grp), cols(half_of(q, h))

        @loop(4)
        def _(i):
            rr = rows(r0 + i * 32, 32)
            dwb[l, rr, cc] = (dwb[l, rr, cc].astype(F32) + rp[q, grp, h, rows(i * 32, 32), :].astype(F32)).astype(BF16)

    def place(q, grp, h, i):
        return rows(block_row(core, q, grp) + C * i, C), cols(half_of(q, h))

    def cp_1(l, q, h, i):
        rr, cc = place(q, 0, h, i)
        return remote(dwb.at[l, rr, cc], r1.at[q, h, i], s_1, v_1.at[q, h, i], nbr[q][0])

    def cp_2(l, q, i):
        rr, cc = place(q, 1, 0, i)
        return remote(dwb.at[l, rr, cc], r2.at[q, i], s_2, v_2.at[q, i], nbr[q][1])

    def fin(q, k, i):
        b1, b2 = bits[q]
        c1 = b1 if k in (0, 1) else flip(b1)
        c2 = b2 if k in (0, 2) else flip(b2)
        return rows(core * H + q * W + c1 * BLK + C * i, C), cols(c2)

    def cp_a(l, q, k, i):
        rr, cc = fin(q, 1 if k == 2 else 0, i)
        return remote(res.at[l, rr, cc], res.at[l, rr, cc], s_a, v_a.at[q, k, i], nbr[q][1 if k == 0 else 0])

    def cp_p(l, q, k, i):
        rr, cc = fin(q, k, i)
        return remote(res.at[l, rr, cc], res.at[l, rr, cc], s_p, v_p, partner)

    QI = [(q, i) for i in TWO for q in TWO]

    def dw_pair(l, who, grp, h):
        for q in TWO:
            dw_block(l, who, q, grp, h)
            if who is not core:
                cp_rp(l, q, grp, h).start()

    def take_rp(l, grp, h):
        pair = rp.at[:, grp, h]
        remote(pair, pair, s_rp, v_rp.at[grp, h], partner).wait_recv()
        for q in TWO:
            add_rp(l, q, grp, h)
            if grp == 0:
                for i in TWO:
                    cp_1(l, q, h, i).start()

    def grads_send(l):
        other = flip(core)
        dw_pair(l, other, 0, 0)
        dw_pair(l, core, 0, 0)
        dw_pair(l, other, 0, 1)
        take_rp(l, 0, 0)
        dw_pair(l, core, 0, 1)
        dw_pair(l, other, 1, 0)
        take_rp(l, 0, 1)
        dw_pair(l, core, 1, 0)
        dw_pair(l, other, 1, 1)
        dw_pair(l, core, 1, 1)

    def recv_1(l, h):
        if h == 0:
            take_rp(l, 1, 0)
            take_rp(l, 1, 1)
        for q, i in QI:
            cp_1(l, q, h, i).wait_recv()
            rr, cc = place(q, 1, h, i)
            dwb[l, rr, cc] = (dwb[l, rr, cc].astype(F32) + r1[q, h, i].astype(F32)).astype(BF16)
            if h == 0:
                cp_2(l, q, i).start()

    def recv_2(l):
        for q, i in QI:
            cp_2(l, q, i).wait_recv()
            rr, cc = fin(q, 0, i)
            res[l, rr, cc] = (dwb[l, rr, cc].astype(F32) + r2[q, i].astype(F32)).astype(BF16)
            cp_a(l, q, 0, i).start()
            cp_p(l, q, 0, i).start()

    def send_a1(l):
        for q, i in QI:
            cp_a(l, q, 1, i).start()

    def recv_a1(l):
        for q, i in QI:
            cp_a(l, q, 0, i).wait_recv()
            cp_a(l, q, 2, i).start()
            cp_p(l, q, 1, i).start()

    def recv_a2(l, k):
        for q, i in QI:
            cp_a(l, q, k, i).wait_recv()
            cp_p(l, q, k + 1, i).start()

    def h_row(who, q):
        return H + who * W + q * BLK

    def dwh_block(who, q, grp):
        lt = hb[2, pl.ds(0, R), rows(h_row(who, q) - H, BLK, BLK)].T
        half = flip(bits[q][0]) if grp == 0 else bits[q][0]
        for n in FOUR:
            dwb[1, rows(h_row(who, q), BLK), pl.ds(pl.multiple_of(half * HALF + n * W, W), W)] = (
                dot(lt, dz[1, 4 * half + n]).astype(BF16))

    def cp_rph(q, grp):
        half = flip(bits[q][0]) if grp == 0 else bits[q][0]
        return remote(dwb.at[1, rows(h_row(flip(core), q), BLK), cols(half)], rph.at[q, grp], s_rph, v_rph.at[grp], partner)

    def quarter(q, grp, h):
        half = flip(bits[q][0]) if grp == 0 else bits[q][0]
        return pl.ds(pl.multiple_of(half * HALF + QTR * half_of(q, h), QTR), QTR)

    def cp_1h(q, h):
        return remote(dwb.at[1, rows(h_row(core, q), BLK), quarter(q, 0, h)], r1h.at[q, h], s_1h, v_1h.at[q, h], nbr[q][0])

    def take_rph(grp):
        pair = rph.at[:, grp]
        remote(pair, pair, s_rph, v_rph.at[grp], partner).wait_recv()
        for q in TWO:
            r0, cc = h_row(core, q), cols(flip(bits[q][0]) if grp == 0 else bits[q][0])

            @loop(4)
            def _(i):
                rr = rows(r0 + i * 32, 32)
                dwb[1, rr, cc] = (dwb[1, rr, cc].astype(F32) + rph[q, grp, rows(i * 32, 32), :].astype(F32)).astype(BF16)
            if grp == 0:
                for h in TWO:
                    cp_1h(q, h).start()

    def grads_send_1():
        for grp in TWO:
            for q in TWO:
                dwh_block(flip(core), q, grp)
                cp_rph(q, grp).start()
            for q in TWO:
                dwh_block(core, q, grp)
            if grp == 0:
                take_rph(0)

    def sum_u():
        remote(hx, hx, s_h, v_h, partner).wait_recv()
        remote(zx, zx, s_z, v_z, partner).wait_recv()
        for m in FOUR:
            f0 = pl.ds(m * BLK, BLK)
            lts = [hb[1, pl.ds(B, R), f0].T] + [hx[i, :, f0].T for i in THREE]
            for n in TWO:
                zs = [dz[1, u_col + n]] + [zx[i, n] for i in THREE]
                acc = None
                for lt, z in zip(lts, zs):
                    p = dot(lt, z).astype(BF16).astype(F32)
                    acc = p if acc is None else acc + p
                ub[f0, W * n:W * n + W] = acc.astype(BF16)

    def item_nbr(j):
        return (u_n1, u_n2) if j < 2 else nbr[j - 2]

    def item_fin(j, k):
        b1, b2 = (u_b1, u_b2) if j < 2 else bits[j - 2]
        c1 = b1 if k in (0, 1) else flip(b1)
        c2 = b2 if k in (0, 2) else flip(b2)
        if j < 2:
            return rows(W * c2 + BLK * j, BLK), pl.ds(pl.multiple_of(core * HALF + QTR * c1, QTR), QTR)
        return rows(h_row(core, j - 2), BLK), pl.ds(pl.multiple_of(HALF * c1 + QTR * c2, QTR), QTR)

    def cp_2x(j):
        if j < 2:
            src, dst = ub.at[rows(W * (flip(u_b2)) + BLK * j, BLK)], r2u.at[j]
        else:
            src, dst = dwb.at[1, rows(h_row(core, j - 2), BLK), quarter(j - 2, 1, 0)], r2h.at[j - 2]
        return remote(src, dst, s_2x, v_2x.at[j], item_nbr(j)[1])

    def cp_ax(j, k):
        rr, cc = item_fin(j, 1 if k == 2 else 0)
        return remote(res.at[1, rr, cc], res.at[1, rr, cc], s_ax, v_ax.at[j if k == 0 else 3 + k], item_nbr(j)[1 if k == 0 else 0])

    def cp_px(j, k):
        rr, cc = item_fin(j, k)
        return remote(res.at[1, rr, cc], res.at[1, rr, cc], s_px, v_px, partner)

    JS = (2, 3, 0, 1)

    def recv_1h(h):
        if h == 0:
            take_rph(1)
        for q in TWO:
            cp_1h(q, h).wait_recv()
            rr, cc = rows(h_row(core, q), BLK), quarter(q, 1, h)
            dwb[1, rr, cc] = (dwb[1, rr, cc].astype(F32) + r1h[q, h].astype(F32)).astype(BF16)
            if h == 0:
                cp_2x(2 + q).start()

    def recv_2x():
        for j in JS:
            cp_2x(j).wait_recv()
            rr, cc = item_fin(j, 0)
            if j < 2:
                mine, got = ub[rows(W * u_b2 + BLK * j, BLK), :], r2u[j]
            else:
                mine, got = dwb[1, rr, cc], r2h[j - 2]
            res[1, rr, cc] = (mine.astype(F32) + got.astype(F32)).astype(BF16)
            cp_ax(j, 0).start()
            cp_px(j, 0).start()

    def send_a1x():
        for j in JS:
            cp_ax(j, 1).start()

    def recv_a1x():
        for j in JS:
            cp_ax(j, 0).wait_recv()
            cp_ax(j, 2).start()
            cp_px(j, 1).start()

    def recv_a2x(k):
        part = res.at[1, pl.ds(0, BLK)]
        remote(part, part, s_ax, v_ax.at[3 + k], partner).wait_recv()
        for j in JS:
            cp_px(j, k + 1).start()

    def between(part):
        if part == 0:
            sum_u()
            for j in TWO:
                cp_2x(j).start()
        else:
            recv_1h(0)

    bwd_layer(1, lambda t: jnp.concatenate([dyv[k, pl.ds(t, B, stride=T), :] for k in FOUR], axis=1), after=lambda r0: send_z(r0, B))
    grads_send_1()

    def put_e(m, v):
        eb[pl.ds(m * W, W), :] = v
    dx_of(1, put_e)
    bwd_layer(0, lambda t: eb[rows(t * B, B), :], between)
    grads_send(0)

    for l in TWO:
        for j in EIGHT:
            dbs[8 * l + j:8 * l + j + 1, :] = jnp.sum(dbacc[l, :, W * j:W * j + W], axis=0, keepdims=True)
    dbb[...] = dbs[...].astype(BF16)
    me = rep * 4 + dat
    cps = [remote(dbb, dbr.at[d - 1], s_db, v_db, dev) for d, dev in enumerate(others, 1)]
    for c in cps:
        c.start()

    def put_dx(m, v):
        for s in EIGHT:
            for k in FOUR:
                dxo[k, pl.ds(8 * m + s, B, stride=T), :] = v[s * B:(s + 1) * B, k * BLK:(k + 1) * BLK]

    recv_1h(1)
    recv_2x()
    dx_of(0, put_dx)
    recv_1(0, 0)
    send_a1x()
    recv_1(0, 1)
    recv_a1x()
    recv_2(0)
    send_a1(0)
    recv_a2x(1)
    recv_a2x(2)
    remote(dbr, dbr, s_db, v_db, partner).wait_recv()
    tot = dbb[...].astype(F32)
    for d in range(7):
        tot += dbr[d].astype(F32)
    dbo[...] = tot
    recv_a1(0)
    recv_a2(0, 1)
    recv_a2(0, 2)
    for n, sem in ((QTR, s_rp), (W, s_1), (BLK, s_2), (384, s_a), (W, s_rph), (BLK, s_1h), (BLK, s_2x), (384, s_ax)):
        part = dwb.at[0, pl.ds(0, n)]
        remote(part, part, sem, v_p, partner).wait_send()
    remote(hx, hx, s_h, v_p, partner).wait_send()
    remote(zx, zx, s_z, v_p, partner).wait_send()
    for l, snd, rcv in ((0, s_p, v_p), (1, s_px, v_px)):
        half_w = res.at[l, pl.ds(0, H)]
        remote(half_w, half_w, snd, rcv, partner).wait()
    remote(dbr, dbr, s_db, v_db, partner).wait_send()


def out_kernel(res, dbo, dxo, dw_ref, db_ref, dx_ref, buf, dbv, sem, xsem):
    cx = [pltpu.make_async_copy(dxo.at[k], dx_ref.at[:, pl.ds(k * BLK, BLK)], xsem.at[k]) for k in FOUR]
    for l in TWO:
        for j in EIGHT:
            dbv[l:l + 1, W * j:W * j + W] = dbo[8 * l + j:8 * l + j + 1, :]
    cx.append(pltpu.make_async_copy(dbv, db_ref, xsem.at[4]))
    for c in cx:
        c.start()
    n = 64

    def cp(s):
        return pltpu.make_async_copy(buf.at[s], dw_ref.at[s // SUB, rows(lax.rem(s, SUB) * n, n)], sem)

    @loop(32)
    def _(s):
        buf[s] = res[s // SUB, rows(lax.rem(s, SUB) * n, n), :].astype(F32)
        cp(s).start()

    pltpu.make_async_copy(buf, buf, sem).wait()
    for c in cx:
        c.wait()


def solution(mesh):
    vm = pl.BlockSpec(memory_space=pltpu.VMEM)
    hbm = pl.BlockSpec(memory_space=pl.ANY)
    dma, vmem = pltpu.SemaphoreType.DMA, pltpu.VMEM

    def local_step(x, dy, w, b):
        scratch = [
            vmem((2, G), F32),
            vmem((4, R, BLK), BF16), vmem((4, B * PAD, BLK), F32), vmem((4, R, BLK), F32),
            vmem((2, 2, 8, H, W), BF16), vmem((2, 2, G, W), BF16), vmem((3, R + B, H), BF16),
            vmem((2, 4, R, H), F32), vmem((2, R + B, H), F32), vmem((2, R, H), F32),
            vmem((2, 8, R, W), BF16), vmem((R, H), F32), vmem((2, 8, G), F32),
            vmem((SUB, W), F32), vmem((SUB, W), BF16), vmem((7, SUB, W), BF16),
            vmem((2, 2 * H, G), BF16), vmem(P3 + (BLK, HALF), BF16),
            vmem(P3 + (C, HALF), BF16), vmem(P2 + (C, HALF), BF16),
            vmem((3, R, H), BF16), vmem((3, 2, R, W), BF16), vmem((H, QTR), BF16),
            vmem(P2 + (BLK, HALF), BF16), vmem(P2 + (BLK, QTR), BF16), vmem((2, BLK, QTR), BF16),
            vmem((2, BLK, QTR), BF16),
            dma((7,)), dma, dma(P2), dma, dma(P3), dma, dma(P2), dma, dma((2, 3, 2)), dma, dma, dma, dma,
            dma, dma, dma, dma, dma, dma((2,)), dma, dma(P2), dma, dma((4,)), dma, dma((6,)), dma, dma,
        ]
        res, dbo, dxo = pl.pallas_call(
            step_kernel,
            out_shape=(vmem((2, 2 * H, G), BF16), vmem((SUB, W), F32), vmem((4, R, BLK), F32)),
            in_specs=[hbm, hbm, hbm, hbm], out_specs=(vm, vm, vm), scratch_shapes=scratch,
            compiler_params=pltpu.CompilerParams(collective_id=0, has_side_effects=True, vmem_limit_bytes=VMEM_LIMIT),
        )(x.reshape(R, H), dy.reshape(R, H), w, b)
        dw, db, dx = pl.pallas_call(
            out_kernel,
            out_shape=(jax.ShapeDtypeStruct((2, 2 * H, G), F32), jax.ShapeDtypeStruct((2, G), F32),
                       jax.ShapeDtypeStruct((R, H), F32)),
            in_specs=[vm, vm, vm], out_specs=(hbm, hbm, hbm),
            scratch_shapes=[vmem((32, 64, G), F32), vmem((2, G), F32), dma, dma((5,))],
            compiler_params=pltpu.CompilerParams(vmem_limit_bytes=32 * HALF * HALF),
        )(res, dbo, dxo)
        return dw, db, dx.reshape(B, T, H)

    rows_spec = P(("replica", "data"))
    return jax.shard_map(local_step, mesh=mesh, in_specs=(rows_spec, rows_spec, P(), P()),
                         out_specs=(P(), P(), rows_spec), check_vma=False)
```

time: 105 us -> 104 us (level)
    pallas_call x1, Pallas kernels: 98 us -> 96.7 us  [local_step(): pl.pallas_call(step_kernel, out_shape=(vmem((2, 2 * H, G), BF16), vmem((S...]
where the time goes in v4:
time: 104 us
  Pallas kernels  103 us (99%)
    pallas_call x1, Pallas kernels, local_step(): pl.pallas_call(step_kernel, out_shape=(vmem((2, 2 * H, G), BF16), vmem((S...  96.7 us
    pallas_call x1, Pallas kernels, local_step(): pl.pallas_call(out_kernel, out_shape=(jax.ShapeDtypeStruct((2, 2 * H, G),...  6.17 us

profile of v4, /device:TPU:0, one launch (start us, length us, event | category | flops | bytes accessed | tf_op | source)
XLA Modules:
  0.0 103.6 jit_solution(11156474630150075377)
XLA Ops:
  0.6 96.7 %shard_map.67 = (bf16[2,1024,2048]{2,1,0:T(8,128)(2,1)S(1)}, f32[16,256]{1,0:T(8,128)S(1)}, f32[4,512,128]{2,1,0:T(8,128)S(1)}) custom-call(bf16[512,512]{1,0:T(8,128)(2,1)} %bitcast.4, f32[512,512]{1,0:T(8,128)} %bitcast.3, bf16[2,1024,2048]{2,1,0:T(8,128)(2,1)} %w_hbm.1, f32[2,2048]{1,0:T(2,128)} %b_hbm.1), custom_call_target="tpu_custom_call" | custom-call | tf_op jit(solution)/shard_map/pallas_call | solution.py:615
  97.3 6.2 %shard_map.68 = (f32[2,1024,2048]{2,1,0:T(8,128)}, f32[2,2048]{1,0:T(2,128)}, f32[512,512]{1,0:T(8,128)}) custom-call(bf16[2,1024,2048]{2,1,0:T(8,128)(2,1)S(1)} %get-tuple-element.9.res, f32[16,256]{1,0:T(8,128)S(1)} %get-tuple-element.10.dbo, f32[4,512,128]{2,1,0:T(8,128)S(1)} %get-tuple-element.11.dxo), custom_call_target="tpu_custom_call" | custom-call | tf_op jit(solution)/shard_map/pallas_call | solution.py:621

commit v5 on v4

--- a/solution.py
+++ b/solution.py
@@ -31,6 +31,14 @@
 
 def dot(a, b):
     return jnp.dot(a, b, preferred_element_type=F32)
+
+
+def dot_k(a, b, k):
+    acc = None
+    for i in range(0, a.shape[1], k):
+        p = dot(a[:, i:i + k], b[i:i + k])
+        acc = p if acc is None else acc + p
+    return acc
 
 
 def dot_nt(a, b):
@@ -113,7 +121,7 @@
             return zin, prod
         for k in (0, 2, 1, 3):
             for n in TWO:
-                prod[2 * k + n] = dot(h, w[l, 1, 2 * k + n])
+                prod[2 * k + n] = dot_k(h, w[l, 1, 2 * k + n], BLK)
         return zin, prod
 
     def step_gates(l, t, zp, c):
@@ -202,10 +210,12 @@
     carry = both(1, carry)
     h0, c0, h1, c1 = both(2, carry, True)
     send_h(7 * 2 * B, 2 * B)
-    for n in EIGHT:
-        in_block(1, 3, n)
     for q in FOUR:
         zp = step_dots(1, 12 + q, h1)
+        if q == 0:
+            for n in EIGHT:
+                in_block(1, 3, n)
+            zp = [gt[1, k, rows(12 * B, B), :] for k in FOUR], zp[1]
         transpose_rec(1, 6 + q // 2, q % 2)
         h1, c1 = step_gates(1, 12 + q, zp, c1)
 
@@ -229,7 +239,7 @@
                 d16 = d.astype(BF16)
                 for n in TWO:
                     dz[l, 2 * k + n, r0, :] = d16[:, W * n:W * n + W]
-                p = [dot(d16, wt[l, n, pl.ds(k * H, H), :]) for n in TWO]
+                p = [dot_k(d16, wt[l, n, pl.ds(k * H, H), :], BLK) for n in TWO]
                 acc = p if acc is None else [a + b for a, b in zip(acc, p)]
             return jnp.concatenate(acc, axis=1), dc * f
 

time: 104 us -> 102 us (0.981)
  Pallas kernels: 103 us -> 101 us
    pallas_call x1, Pallas kernels: 96.7 us -> 95.1 us  [local_step(): pl.pallas_call(step_kernel, out_shape=(vmem((2, 2 * H, G), BF16), vmem((S...]
where the time goes in v5:
time: 102 us
  Pallas kernels  101 us (99%)
    pallas_call x1, Pallas kernels, local_step(): pl.pallas_call(step_kernel, out_shape=(vmem((2, 2 * H, G), BF16), vmem((S...  95.1 us
    pallas_call x1, Pallas kernels, local_step(): pl.pallas_call(out_kernel, out_shape=(jax.ShapeDtypeStruct((2, 2 * H, G),...  6.17 us

profile of v5, /device:TPU:0, one launch (start us, length us, event | category | flops | bytes accessed | tf_op | source)
XLA Modules:
  0.0 102.0 jit_solution(11242352550865848616)
XLA Ops:
  0.6 95.1 %shard_map.67 = (bf16[2,1024,2048]{2,1,0:T(8,128)(2,1)S(1)}, f32[16,256]{1,0:T(8,128)S(1)}, f32[4,512,128]{2,1,0:T(8,128)S(1)}) custom-call(bf16[512,512]{1,0:T(8,128)(2,1)} %bitcast.4, f32[512,512]{1,0:T(8,128)} %bitcast.3, bf16[2,1024,2048]{2,1,0:T(8,128)(2,1)} %w_hbm.1, f32[2,2048]{1,0:T(2,128)} %b_hbm.1), custom_call_target="tpu_custom_call" | custom-call | tf_op jit(solution)/shard_map/pallas_call | solution.py:625
  95.7 6.2 %shard_map.68 = (f32[2,1024,2048]{2,1,0:T(8,128)}, f32[2,2048]{1,0:T(2,128)}, f32[512,512]{1,0:T(8,128)}) custom-call(bf16[2,1024,2048]{2,1,0:T(8,128)(2,1)S(1)} %get-tuple-element.9.res, f32[16,256]{1,0:T(8,128)S(1)} %get-tuple-element.10.dbo, f32[4,512,128]{2,1,0:T(8,128)S(1)} %get-tuple-element.11.dxo), custom_call_target="tpu_custom_call" | custom-call | tf_op jit(solution)/shard_map/pallas_call | solution.py:631

commit v6 on v5

--- a/solution.py
+++ b/solution.py
@@ -145,6 +145,24 @@
         return jnp.concatenate(hs, axis=1), jnp.concatenate(cs, axis=1)
 
     zero_state = (jnp.zeros((B, H), BF16), jnp.zeros((B, H), F32))
+    def pick(a, b):
+        return a + core * (b - a)
+
+    u_b1, u_b2 = pick(mx, rep), pick(rep, mx)
+    u_n1 = (pick(rep, flip(rep)), pick(lax.rem(dat + 2, 4), dat))
+    u_n2 = (pick(flip(rep), rep), pick(dat, lax.rem(dat + 2, 4)))
+    x_core0, y_core1 = (rep, 2 * (flip(mx))), (flip(rep), 2 * mx + 1)
+    dests = ((partner, 0, pick(4 + 2 * rep, 2 * mx)), (x_core0, 1 + core, 2 * (flip(mx))), (y_core1, 1 + core, 4 + 2 * (flip(rep))))
+    u_col = pick(2 * mx, 4 + 2 * rep)
+
+    def send_h(r0, n):
+        for dev, slot, _ in dests:
+            remote(hb.at[1, rows(B + r0, n)], hx.at[slot, rows(r0, n)], s_h, v_h, dev).start()
+
+    def send_z(r0, n):
+        for dev, slot, c0 in dests:
+            remote(dz.at[1, pl.ds(c0, 2), rows(r0, n)], zx.at[slot, :, rows(r0, n)], s_z, v_z, dev).start()
+
     for n in EIGHT:
         in_block(0, 0, n)
     h0, c0 = None, zero_state[1]
@@ -162,33 +180,17 @@
         if q == 1:
             transpose_rec(0, 0, 0)
         h0, c0 = step_gates(0, q, zp, c0)
+        if q == 1:
+            pl.semaphore_wait(barrier, 7)
+            send_h(0, 2 * B)
     wait_w(1, 0)
     wait_w(1, 1)
 
-    def pick(a, b):
-        return a + core * (b - a)
-
-    u_b1, u_b2 = pick(mx, rep), pick(rep, mx)
-    u_n1 = (pick(rep, flip(rep)), pick(lax.rem(dat + 2, 4), dat))
-    u_n2 = (pick(flip(rep), rep), pick(dat, lax.rem(dat + 2, 4)))
-    x_core0, y_core1 = (rep, 2 * (flip(mx))), (flip(rep), 2 * mx + 1)
-    dests = ((partner, 0, pick(4 + 2 * rep, 2 * mx)), (x_core0, 1 + core, 2 * (flip(mx))), (y_core1, 1 + core, 4 + 2 * (flip(rep))))
-    u_col = pick(2 * mx, 4 + 2 * rep)
-
-    def send_h(r0, n):
-        for dev, slot, _ in dests:
-            remote(hb.at[1, rows(B + r0, n)], hx.at[slot, rows(r0, n)], s_h, v_h, dev).start()
-
-    def send_z(r0, n):
-        for dev, slot, c0 in dests:
-            remote(dz.at[1, pl.ds(c0, 2), rows(r0, n)], zx.at[slot, :, rows(r0, n)], s_z, v_z, dev).start()
-
-    pl.semaphore_wait(barrier, 7)
-
-    def both(s, carry, last=False):
+    def both(s, carry, first=False, last=False):
         h0, c0, h1, c1 = carry
         t0, t1 = 4 * s + 4, 4 * s
-        send_h(s * BLK, BLK)
+        if first:
+            send_h(2 * B, 2 * B)
         a = step_dots(0, t0, h0)
         for n in EIGHT:
             in_block(1, s, n)
@@ -202,14 +204,13 @@
             transpose_rec(0, 2 * s + 2 + q // 2, q % 2)
             transpose_rec(1, 2 * s + q // 2, q % 2)
             h1, c1 = step_gates(1, t1 + q, b, c1)
-            if last and q == MID:
-                send_h(6 * 2 * B, 2 * B)
+            if q == MID:
+                send_h(t0 * B, BLK)
         return h0, c0, h1, c1
 
-    carry = both(0, (h0, c0, None, zero_state[1]))
+    carry = both(0, (h0, c0, None, zero_state[1]), first=True)
     carry = both(1, carry)
-    h0, c0, h1, c1 = both(2, carry, True)
-    send_h(7 * 2 * B, 2 * B)
+    h0, c0, h1, c1 = both(2, carry, last=True)
     for q in FOUR:
         zp = step_dots(1, 12 + q, h1)
         if q == 0:

time: 102 us -> 102 us (level)
  no operation moved by 1% of the time
where the time goes in v6:
time: 102 us
  Pallas kernels  101 us (99%)
    pallas_call x1, Pallas kernels, local_step(): pl.pallas_call(step_kernel, out_shape=(vmem((2, 2 * H, G), BF16), vmem((S...  94.6 us
    pallas_call x1, Pallas kernels, local_step(): pl.pallas_call(out_kernel, out_shape=(jax.ShapeDtypeStruct((2, 2 * H, G),...  6.17 us

profile of v6, /device:TPU:0, one launch (start us, length us, event | category | flops | bytes accessed | tf_op | source)
XLA Modules:
  0.0 101.5 jit_solution(10384493774334821794)
XLA Ops:
  0.6 94.6 %shard_map.67 = (bf16[2,1024,2048]{2,1,0:T(8,128)(2,1)S(1)}, f32[16,256]{1,0:T(8,128)S(1)}, f32[4,512,128]{2,1,0:T(8,128)S(1)}) custom-call(bf16[512,512]{1,0:T(8,128)(2,1)} %bitcast.4, f32[512,512]{1,0:T(8,128)} %bitcast.3, bf16[2,1024,2048]{2,1,0:T(8,128)(2,1)} %w_hbm.1, f32[2,2048]{1,0:T(2,128)} %b_hbm.1), custom_call_target="tpu_custom_call" | custom-call | tf_op jit(solution)/shard_map/pallas_call | solution.py:626
  95.2 6.2 %shard_map.68 = (f32[2,1024,2048]{2,1,0:T(8,128)}, f32[2,2048]{1,0:T(2,128)}, f32[512,512]{1,0:T(8,128)}) custom-call(bf16[2,1024,2048]{2,1,0:T(8,128)(2,1)S(1)} %get-tuple-element.9.res, f32[16,256]{1,0:T(8,128)S(1)} %get-tuple-element.10.dbo, f32[4,512,128]{2,1,0:T(8,128)S(1)} %get-tuple-element.11.dxo), custom_call_target="tpu_custom_call" | custom-call | tf_op jit(solution)/shard_map/pallas_call | solution.py:632
